TPU v7x, 256 devices: a whole 4x4x8 slice. The times are simulated.
256 devices in a mesh: seq: 64 (over x, z, core), head: 4 (over y).
Axes of the slice: x: 4, y: 4, z: 8, core: 2. Of those that a mesh axis runs over, the one named last changes fastest.
Arguments:
- queries: bfloat16 [32768, 1024], P('seq', 'head'), may hold values from -6 to 6
- key_vectors: bfloat16 [32768, 1024], P('seq', 'head'), may hold values from -6 to 6
- values: bfloat16 [32768, 2048], P('seq', 'head'), may hold values from -6 to 6
- log_gate: bfloat16 [32768, 1024], P('seq', 'head'), may hold values from -1.6 to 0, as said below
- out_gate: bfloat16 [32768, 2048], P('seq', 'head'), may hold values from -6 to 6
- norm_gain: float32 [2048], P('head'), may hold values from 0.5 to 1.5
- out_weight: bfloat16 [2048, 2048], P('head'), may hold values from -0.1875 to 0.1875
Outputs:
- mixed: bfloat16 [32768, 2048], P('seq', 'head')
Inputs may be any that keep to these rules, and one draw needn't show every extreme that they name: `log_gate`: every entry is below zero.
All inputs are finite; a program needn't handle non-finite values.
Results may differ from a plain program's by a relative error of at most 0.017.
Values may be sent and summed in bfloat16 or wider, within the bound.
A program may use at most 128 MiB of HBM per device.

v0:
```python
import jax
import jax.numpy as jnp
from jax import lax
from jax.sharding import Mesh
from jax.sharding import PartitionSpec as P

DK = 256
DV = 512
SPAN = 64
SEQ = ("seq_0", "seq_1", "seq_2")


def nothing_yet(shard, identity):
    return jax.tree.map(
        lambda part, zero: jnp.zeros_like(part) + jnp.asarray(zero, part.dtype), shard, identity
    )


def prefix_by_axis(shard, axes, combine, identity):
    before = start = nothing_yet(shard, identity)
    subtotal = shard
    for axis in reversed(axes):
        length, position = (lax.axis_size(axis), lax.axis_index(axis))
        pieces = jax.tree.map(
            lambda part, kind: lax.all_gather(part.astype(kind), axis),
            subtotal,
            (jnp.bfloat16, jnp.bfloat16),
        )
        inside, subtotal = (start, start)
        for k in range(length):
            passed = k < position
            subtotal = combine(
                subtotal, jax.tree.map(lambda part, own: part[k].astype(own.dtype), pieces, shard)
            )
            inside = jax.tree.map(lambda new, old: jnp.where(passed, new, old), subtotal, inside)
        before = combine(inside, before)
    return before


def cut_along(shard, dim, length):
    before, after = (shard.shape[:dim], shard.shape[dim + 1 :])
    return jnp.moveaxis(shard.reshape(*before, length, -1, *after), dim, 0)


def summed_on_arrival(shard, axis, dim):
    length = lax.axis_size(axis)
    parts = lax.all_to_all(cut_along(shard, dim, length), axis, 0, 0, tiled=True)
    return jnp.sum(parts.astype(jnp.float32), axis=0)


def join_states(earlier, latter):
    return (earlier[0] + latter[0], jnp.exp(latter[0])[..., None, :] * earlier[1] + latter[1])


def shards(queries, key_vectors, values, log_gate, out_gate, norm_gain, out_weight):
    length = queries.shape[0]
    head_count = queries.shape[1] // DK
    blocks = length // SPAN
    middle_pos = SPAN // 2
    running = jnp.cumsum(log_gate.astype(jnp.float32).reshape(blocks, SPAN, head_count, DK), axis=1)
    middle = running[:, middle_pos : middle_pos + 1]
    ending = running[:, SPAN - 1 : SPAN]
    query_f = queries.reshape(blocks, SPAN, head_count, DK).astype(jnp.float32)
    key_f = key_vectors.reshape(blocks, SPAN, head_count, DK).astype(jnp.float32)
    q_inter = (query_f * jnp.exp(running)).astype(jnp.bfloat16)
    q_intra = (query_f * jnp.exp(running - middle)).astype(jnp.bfloat16)
    k_intra = (key_f * jnp.exp(middle - running)).astype(jnp.bfloat16)
    k_state = (key_f * jnp.exp(ending - running)).astype(jnp.bfloat16)
    value_blocks = values.reshape(blocks, SPAN, head_count, DV)
    block_state = jnp.einsum(
        "bthe,bthd->bhed", value_blocks, k_state, preferred_element_type=jnp.float32
    )
    block_log = ending[:, 0]
    run_log, run_state = lax.associative_scan(join_states, (block_log, block_state), axis=0)
    device_log = run_log[-1]
    device_state = run_state[-1]
    before_log = run_log - block_log
    before_state = jnp.concatenate([jnp.zeros_like(run_state[:1]), run_state[:-1]], axis=0)
    scores = jnp.einsum("bthd,bshd->bhts", q_intra, k_intra, preferred_element_type=jnp.float32)
    causal = lax.iota(jnp.int32, SPAN)[:, None] >= lax.iota(jnp.int32, SPAN)[None, :]
    weights = jnp.where(causal, scores, 0.0).astype(jnp.bfloat16)
    local_part = jnp.einsum(
        "bhts,bshe->bthe", weights, value_blocks, preferred_element_type=jnp.float32
    )
    zero_log = jnp.zeros_like(device_log)
    zero_state = jnp.zeros_like(device_state)
    incoming_log, incoming = prefix_by_axis(
        (device_log, device_state), SEQ, join_states, (zero_log, zero_state)
    )
    carried = jnp.exp(before_log)[..., None, :] * incoming[None] + before_state
    carried_low = carried.astype(jnp.bfloat16)
    carried_part = jnp.einsum(
        "bthd,bhed->bthe", q_inter, carried_low, preferred_element_type=jnp.float32
    )
    attention = local_part + carried_part
    spread = jnp.mean(attention * attention, axis=-1, keepdims=True)
    normed = attention * lax.rsqrt(spread + 1e-05) * norm_gain.reshape(head_count, DV)
    outer_f = out_gate.reshape(blocks, SPAN, head_count, DV).astype(jnp.float32)
    gated_out = (normed * jax.nn.silu(outer_f)).astype(jnp.bfloat16)
    partial_value = jnp.dot(
        gated_out.reshape(length, head_count * DV), out_weight, preferred_element_type=jnp.float32
    )
    return summed_on_arrival(partial_value.astype(jnp.bfloat16), "head", 1).astype(jnp.bfloat16)


def solution(mesh):
    split = Mesh(
        mesh.devices.reshape(4, 8, 2, mesh.shape["head"]), ("seq_0", "seq_1", "seq_2", "head")
    )
    in_specs = (
        P(SEQ, "head"),
        P(SEQ, "head"),
        P(SEQ, "head"),
        P(SEQ, "head"),
        P(SEQ, "head"),
        P("head"),
        P("head", None),
    )
    out_specs = P(SEQ, "head")
    return jax.shard_map(
        shards, mesh=split, in_specs=in_specs, out_specs=out_specs, check_vma=False
    )
```

profile of v0, /device:TPU:2, one launch (start us, length us, event | category | flops | bytes accessed | tf_op | source)
XLA Modules:
  0.0 164.7 jit_solution(14921206279857943041)
XLA Ops:
  6.5 1.1 convert.16
  8.4 1.8 %all_gather.24 = bf16[2,1,256]{2,1,0:T(2,128)(2,1)S(1)} all-gather(bf16[1,1,256]{2,1,0:T(2,128)(2,1)S(1)} %fusion.54), channel_id=1, replica_groups=mesh['seq_0'=4,'seq_1'=8,'seq_2'=2,'head'=4] {'seq_2'}, dimensions={0}, use_global_device_ids=true | all-gather | bytes 1536 | tf_op jit(solution)/shard_map/all_gather | solution.py:25
  10.3 1.5 fusion.29
  11.9 0.8 fusion.37
  12.9 1.7 %copy-done.1 = f32[8,256,512]{2,1,0:T(8,128)} copy-done((f32[8,256,512]{2,1,0:T(8,128)}, f32[8,256,512]{2,1,0:T(8,128)S(1)}, u32[]{:S(2)}) %copy-start.1) | copy-done | bytes 4194328
  15.1 1.1 pad_maximum_fusion.1
  16.2 3.5 %pad.47 = f32[4,1,512,256]{2,3,0,1:T(8,128)} pad(f32[2,1,512,256]{2,3,0,1:T(8,128)} %pad_maximum_fusion.1, f32[]{:T(128)} %constant.18.clone.1), padding=0_1_1x0_0_0x0_0_0x0_0_0 | pad | bytes 3145732 | tf_op jit(solution)/shard_map/pad | solution.py:74
  19.7 2.4 %pad.48 = f32[4,1,512,256]{2,3,0,1:T(8,128)} pad(f32[2,1,512,256]{2,3,0,1:T(8,128)S(1)} %pad_add_fusion, f32[]{:T(128)} %constant.18.clone.1), padding=1_0_1x0_0_0x0_0_0x0_0_0 | pad | bytes 3145732 | tf_op jit(solution)/shard_map/pad | solution.py:74
  22.0 4.0 %add.317 = f32[4,1,512,256]{2,3,0,1:T(8,128)} add(f32[4,1,512,256]{2,3,0,1:T(8,128)} %pad.47, f32[4,1,512,256]{2,3,0,1:T(8,128)} %pad.48) | non-fusion elementwise | flops 524288 | bytes 6291456 | tf_op jit(solution)/shard_map/add | solution.py:74
  26.1 5.7 %pad.93 = f32[8,1,512,256]{2,3,0,1:T(8,128)} pad(f32[4,1,512,256]{2,3,0,1:T(8,128)} %add.317, f32[]{:T(128)} %constant.18.clone.1), padding=1_0_1x0_0_0x0_0_0x0_0_0 | pad | bytes 6291460
  31.8 2.6 %fusion.5 = f32[3,1,512,256]{2,3,0,1:T(8,128)S(1)} fusion(f32[4,1,512,256]{2,3,0,1:T(8,128)} %pad.48, f32[4,1,512,256]{2,3,0,1:T(8,128)} %pad.47, f32[8,1,512,256]{2,3,0,1:T(8,128)} %bitcast.111, f32[3,256]{1,0:T(4,128)S(1)} %get-tuple-element.34), kind=kLoop, calls=%fused_computation.10 | loop fusion | flops 1179648 | bytes 6294528 | tf_op jit(solution)/shard_map/add | solution.py:52
  34.4 1.1 slice_bitcast_fusion
  35.5 1.5 pad_maximum_fusion
  37.0 5.8 %pad.49 = f32[8,1,512,256]{2,3,0,1:T(8,128)} pad(f32[4,1,512,256]{2,3,0,1:T(8,128)} %pad_maximum_fusion, f32[]{:T(128)} %constant.18.clone.1), padding=0_1_1x0_0_0x0_0_0x0_0_0 | pad | bytes 6291460 | tf_op jit(solution)/shard_map/pad | solution.py:74
  42.8 1.3 add_convert_fusion.1
  44.2 2.2 %all_gather.27 = bf16[2,1,512,256]{3,2,1,0:T(8,128)(2,1)S(1)} all-gather(bf16[1,1,512,256]{3,2,1,0:T(8,128)(2,1)S(1)} %copy.28), channel_id=1, replica_groups=mesh['seq_0'=4,'seq_1'=8,'seq_2'=2,'head'=4] {'seq_2'}, dimensions={0}, use_global_device_ids=true | all-gather | bytes 786432 | tf_op jit(solution)/shard_map/all_gather | solution.py:25
  46.3 0.8 fusion.35
  47.2 19.2 %all_gather.25 = bf16[8,1,256]{2,1,0:T(2,128)(2,1)S(1)} all-gather(bf16[1,1,256]{2,1,0:T(2,128)(2,1)S(1)} %get-tuple-element.41), channel_id=1, replica_groups=mesh['seq_0'=4,'seq_1'=8,'seq_2'=2,'head'=4] {'seq_1'}, dimensions={0}, use_global_device_ids=true | all-gather | bytes 4608 | tf_op jit(solution)/shard_map/all_gather | solution.py:25
  66.4 24.7 %all-gather.3.cloned.1.call-done = bf16[8,1,512,256]{3,2,1,0:T(8,128)(2,1)} async-done(((bf16[1,1,512,256]{3,2,1,0:T(8,128)(2,1)}), bf16[8,1,512,256]{3,2,1,0:T(8,128)(2,1)}) %all-gather.3.cloned.1.call-update) | async-done | bytes 2097168 | tf_op jit(solution)/shard_map/all_gather | solution.py:25
  91.1 2.6 %fusion.34 = bf16[1,1,512,256]{3,2,1,0:T(8,128)(2,1)} fusion(f32[256]{0:T(256)S(1)} %bitcast.140, f32[256]{0:T(256)S(1)} %bitcast.128, f32[256]{0:T(256)S(1)} %bitcast.126, f32[256]{0:T(256)S(1)} %bitcast.138, f32[256]{0:T(256)S(1)} %bitcast.136, f32[256]{0:T(256)S(1)} %bitcast.134, f32[256]{0:T(256)S(1)} %bitcast.132, f32[256]{0:T(256)S(1)} %bitcast.130, ...), kind=kLoop, calls=%fused_computation.54 | loop fusion | flops 3145728 | bytes 2367488 | tf_op jit(solution)/shard_map/convert_element_type | solution.py:25
  93.8 5.6 %pad.61 = f32[7,1,512,256]{2,3,0,1:T(8,128)} pad(f32[4,1,512,256]{2,3,0,1:T(8,128)} %pad_maximum_fusion, f32[]{:T(128)} %constant.18.clone.1), padding=0_0_1x0_0_0x0_0_0x0_0_0 | pad | bytes 5767172 | tf_op jit(solution)/shard_map/slice | solution.py:78
  99.5 7.8 %all_gather.26 = bf16[4,1,256]{2,1,0:T(2,128)(2,1)S(1)} all-gather(bf16[1,1,256]{2,1,0:T(2,128)(2,1)S(1)} %get-tuple-element.20), channel_id=1, replica_groups=mesh['seq_0'=4,'seq_1'=8,'seq_2'=2,'head'=4] {'seq_0'}, dimensions={0}, use_global_device_ids=true | all-gather | bytes 2560 | tf_op jit(solution)/shard_map/all_gather | solution.py:25
  107.3 0.7 exponential_bitcast_fusion
  108.0 2.4 %convolution_bitcast_fusion = f32[8,512,64]{1,2,0:T(8,128)} fusion(bf16[8,64,512]{2,1,0:T(8,128)(2,1)S(1)} %bitcast.116, bf16[8,64,256]{2,0,1:T(8,128)(2,1)} %get-tuple-element.14, bf16[8,64,256]{2,0,1:T(8,128)(2,1)} %get-tuple-element.15, pred[64,64]{1,0:T(8,128)(4,1)S(1)} %iota_compare_fusion), kind=kOutput, calls=%fused_computation.13 | convolution fusion | flops 50397184 | bytes 2101248 | tf_op jit(solution)/shard_map/bhts,bshe->bthe/dot_general | solution.py:82
  110.5 5.8 %slice_add_fusion.4 = f32[7,1,512,256]{2,3,0,1:T(8,128)} fusion(f32[7,1,512,256]{2,3,0,1:T(8,128)} %pad.61, f32[8,1,512,256]{2,3,0,1:T(8,128)} %pad.93), kind=kLoop, calls=%fused_computation.153 | loop fusion | flops 917504 | bytes 11010048 | tf_op jit(solution)/shard_map/add | solution.py:74
  116.3 1.7 %all-gather.5.cloned.1.call-done = bf16[4,1,512,256]{3,2,1,0:T(8,128)(2,1)} async-done(((bf16[1,1,512,256]{3,2,1,0:T(8,128)(2,1)}), bf16[4,1,512,256]{3,2,1,0:T(8,128)(2,1)}) %all-gather.5.cloned.1.call-update) | async-done | bytes 1048592 | tf_op jit(solution)/shard_map/all_gather | solution.py:25
  118.0 2.8 %add_bitcast_fusion = f32[512,256]{1,0:T(8,128)S(1)} fusion(bf16[4,1,512,256]{3,2,1,0:T(8,128)(2,1)} %all-gather.5.cloned.1.call-done, f32[256]{0:T(256)S(1)} %bitcast.145, f32[256]{0:T(256)S(1)} %bitcast.125, f32[256]{0:T(256)S(1)} %bitcast.123, f32[256]{0:T(256)S(1)} %bitcast.141, f32[256]{0:T(256)S(1)} %bitcast.129, f32[256]{0:T(256)S(1)} %bitcast.127, ...), kind=kLoop, calls=%fused_computation.52 | loop fusion | flops 7471104 | bytes 4210702 | tf_op jit(solution)/shard_map/mul | solution.py:90
  121.0 3.2 %multiply_reduce_fusion = (f32[8,64]{1,0:T(8,128)S(1)}, f32[8,1,512,64]{2,3,0,1:T(8,128)S(1)}) fusion(f32[8,512,64]{1,2,0:T(8,128)} %convolution_bitcast_fusion, f32[7,1,512,256]{2,3,0,1:T(8,128)} %slice_add_fusion.4, f32[512,256]{0,1:T(8,128)S(1)} %copy.29, f32[8,256]{1,0:T(8,128)S(1)} %exponential_bitcast_fusion, ...), kind=kOutput, calls=%fused_computation.26 | convolution fusion | flops 138149376 | bytes 6563840 | tf_op jit(solution)/shard_map/bthd,bhed->bthe/dot_general | solution.py:92
  124.3 0.4 fusion.17
  124.6 1.3 convolution_convert_fusion
  126.1 28.9 %all_to_all.5 = bf16[4,512,512]{2,1,0:T(8,128)(2,1)} all-to-all(bf16[4,512,512]{2,1,0:T(8,128)(2,1)S(1)} %bitcast.113), channel_id=1, replica_groups=mesh['seq_0'=4,'seq_1'=8,'seq_2'=2,'head'=4] {'head'}, dimensions={0} | all-to-all | bytes 4194304 | tf_op jit(solution)/shard_map/all_to_all | solution.py:47
  155.0 2.9 %reduce_sum.22 = bf16[512,512]{1,0:T(8,128)(2,1)} reduce(bf16[4,512,512]{2,1,0:T(8,128)(2,1)} %all_to_all.5, bf16[]{:T(256)} %constant.48.clone.1), dimensions={0}, to_apply=%region_2.3 | reduce | flops 786432 | bytes 2621442 | tf_op jit(solution)/shard_map/reduce_sum | solution.py:48
  (60 shorter events, 2.2 us)
Async XLA Ops:
  6.5 118.1 %copy-start = (bf16[512,2048]{1,0:T(8,128)(2,1)S(1)}, bf16[512,2048]{1,0:T(8,128)(2,1)}, u32[]{:S(2)}) copy-start(bf16[512,2048]{1,0:T(8,128)(2,1)} %param.13) | copy-start | bytes 6291460
  6.5 3.7 %copy-start.6 = (bf16[512,256]{1,0:T(8,128)(2,1)S(1)}, bf16[512,256]{1,0:T(8,128)(2,1)}, u32[]{:S(2)}) copy-start(bf16[512,256]{1,0:T(8,128)(2,1)} %param.8) | copy-start | bytes 786436
  6.5 3.7 %copy-start.7 = (bf16[512,256]{1,0:T(8,128)(2,1)S(1)}, bf16[512,256]{1,0:T(8,128)(2,1)}, u32[]{:S(2)}) copy-start(bf16[512,256]{1,0:T(8,128)(2,1)} %param.7) | copy-start | bytes 786436
  6.5 84.6 %all-gather.3.cloned.1.call-start = ((), (), s32[]{:S(2)}) async-start(), calls=%async_computation.1 | async-start | bytes 2359296 | tf_op jit(solution)/shard_map/all_gather | solution.py:25
  8.1 3.8 %copy-start.2 = (f32[8,64,1,256]{3,0,1,2:T(8,128)}, f32[8,64,1,256]{3,0,1,2:T(8,128)S(1)}, u32[]{:S(2)}) copy-start(f32[8,64,1,256]{3,0,1,2:T(8,128)S(1)} %fusion.32) | copy-start | bytes 1572868
  10.2 1.7 %copy-start.3 = (bf16[512,512]{1,0:T(8,128)(2,1)S(1)}, bf16[512,512]{1,0:T(8,128)(2,1)}, u32[]{:S(2)}) copy-start(bf16[512,512]{1,0:T(8,128)(2,1)} %param.9) | copy-start | bytes 1572868
  12.6 2.0 %copy-start.1 = (f32[8,256,512]{2,1,0:T(8,128)}, f32[8,256,512]{2,1,0:T(8,128)S(1)}, u32[]{:S(2)}) copy-start(f32[8,256,512]{2,1,0:T(8,128)S(1)} %fusion.37) | copy-start | bytes 12582916
  47.2 70.8 %all-gather.5.cloned.1.call-start = ((), (), s32[]{:S(2)}) async-start(), calls=%async_computation.2 | async-start | bytes 1310720 | tf_op jit(solution)/shard_map/all_gather | solution.py:25
  93.8 14.2 %copy-start.4 = (bf16[512,512]{1,0:T(8,128)(2,1)S(1)}, bf16[512,512]{1,0:T(8,128)(2,1)}, u32[]{:S(2)}) copy-start(bf16[512,512]{1,0:T(8,128)(2,1)} %param.9) | copy-start | bytes 1572868
  121.0 3.2 %copy-start.5 = (bf16[512,512]{1,0:T(8,128)(2,1)S(1)}, bf16[512,512]{1,0:T(8,128)(2,1)}, u32[]{:S(2)}) copy-start(bf16[512,512]{1,0:T(8,128)(2,1)} %param.11) | copy-start | bytes 1572868
  121.0 3.2 %copy-start.8 = (f32[512]{0:T(512)S(1)}, f32[512]{0:T(512)}, u32[]{:S(2)}) copy-start(f32[512]{0:T(512)} %param.12) | copy-start | bytes 6148
Sparse Core Ops, SparseCore 0:
  47.3 43.7 all-gather.2
  93.9 24.0 all-gather.4
where the time goes:
time: 166 us; the launch traced here: 165 us
  blocking collectives  59.9 us (36%)
  other arithmetic  30.5 us (18%)
  local copies, waits for them, and re-layouts  26.4 us (16%)
  waiting for transfers between devices  26.4 us (16%)
  between operations  13.7 us (8%)
  matrix products  7.64 us (5%)
    all_gather x4, blocking collectives, prefix_by_axis(): lax.all_gather(part.astype(kind), axis)  31 us
    all_to_all x1, blocking collectives, summed_on_arrival(): lax.all_to_all(cut_along(shard, dim, length), axis, 0, 0, tiled=True)  28.9 us
    all_gather x2, waiting for transfers between devices, prefix_by_axis(): lax.all_gather(part.astype(kind), axis)  26.4 us
    pad x7, local copies, waits for them, and re-layouts, shards(): lax.associative_scan(join_states, (block_log, block_state), axis=0)  11.7 us
    add x5, other arithmetic, shards(): lax.associative_scan(join_states, (block_log, block_state), axis=0)  9.96 us
    unnamed x19, local copies, waits for them, and re-layouts  7.46 us
    slice x1, local copies, waits for them, and re-layouts, shards(): run_state[:-1]  5.59 us
    mul x2, other arithmetic, shards(): carried = jnp.exp(before_log)[..., None, :] * incoming[None] + before_state  3.52 us
  transfers between devices with their start and end apart: 2, of which 2 were waited for; matrix products, arithmetic and copies ran while one was open for 9% of the time, Pallas kernels for 0%

commit v1 on v0

v1 whole, which is shorter than its diff:
```python
import functools

import jax
import jax.numpy as jnp
from jax import lax
from jax.experimental import pallas as pl
from jax.experimental.pallas import tpu as pltpu
from jax.sharding import Mesh
from jax.sharding import PartitionSpec as P

DK = 256
DV = 512
SPAN = 64
X, Z, C, Y = ("seq_0", "seq_1", "seq_2", "head")
SEQ = (X, Z, C)
F32 = jnp.float32
BF16 = jnp.bfloat16
MESH_ID = pl.DeviceIdType.MESH


def mm(a, b):
    return lax.dot_general(a, b, (((1,), (0,)), ((), ())), preferred_element_type=F32)


def mm_nt(a, b):
    return lax.dot_general(a, b, (((1,), (1,)), ((), ())), preferred_element_type=F32)


def mm_tn(a, b):
    return lax.dot_general(a, b, (((0,), (0,)), ((), ())), preferred_element_type=F32)


def remote(src, dst, send, recv, where):
    return pltpu.make_async_remote_copy(
        src_ref=src, dst_ref=dst, send_sem=send, recv_sem=recv,
        device_id=where, device_id_type=MESH_ID,
    )


def far_first(n):
    return sorted(range(1, n), key=lambda d: (-min(d, n - d), d))


def near_first(n):
    return sorted(range(1, n), key=lambda d: (min(d, n - d), d))


def body(
    nx, nz, tok, width,
    q_hbm, k_hbm, v_hbm, g_hbm, og_hbm, gain_hbm, w_hbm, out_hbm,
    q_v, k_v, v_v, g_v, og_v, gain_v, w_v,
    run_v, kd_v, qa_v, ka_v, b_v, c_v, d_v, q0_v, qp_v, wgt_v, wd_v, loc_v, gate_v,
    es_v, er_v, ss_v, sr_v, own_v,
    lzs_v, lz_v, zs_v, zr_v, pre_v, lxs_v, lx_v, xs_v, xr_v, zb_v, inc_v,
    ps_v, pr_v, k0_v, k1_v, p2s_v, p2r_v, o_v,
    in_sem, out_sem, e_sem, s_sem, lz_sem, z_sem, lx_sem, x_sem, b_sem, f_sem, p_sem, p2_sem,
):
    x, z, c, y = (lax.axis_index(n) for n in (X, Z, C, Y))
    half = DV // 2
    piece = half // nz
    y_a = y + 1 - 2 * (y % 2)
    y_b = 3 - y
    other = {C: 1 - c}

    barrier = pltpu.get_barrier_semaphore()
    peers = [other, {Y: y_a}, {Y: y_b}]
    peers += [{Z: (z + d) % nz} for d in range(1, nz)]
    peers += [{X: (x + d) % nx} for d in range(1, nx)]
    for peer in peers:
        pl.semaphore_signal(barrier, inc=1, device_id=peer, device_id_type=MESH_ID)

    loads = []
    for i, (src, dst) in enumerate((
        (g_hbm, g_v), (k_hbm, k_v), (v_hbm, v_v), (q_hbm, q_v),
        (og_hbm, og_v), (gain_hbm, gain_v), (w_hbm, w_v),
    )):
        copy = pltpu.make_async_copy(src, dst, in_sem.at[i])
        copy.start()
        loads.append(copy)
    load_g, load_k, load_v, load_q, load_og, load_gain, load_w = loads

    group = 256
    tri = (
        lax.broadcasted_iota(jnp.int32, (group, group), 0)
        >= lax.broadcasted_iota(jnp.int32, (group, group), 1)
    ).astype(BF16)
    load_g.wait()
    carry = jnp.zeros((1, DK), F32)
    for h in range(tok // group):
        rows = slice(h * group, (h + 1) * group)
        part = mm(tri, g_v[rows, :]) + carry
        run_v[rows, :] = part
        carry = part[group - 1:group, :]
    total = carry
    es_v[...] = jnp.broadcast_to(total, es_v.shape)

    pl.semaphore_wait(barrier, len(peers))
    e_copy = remote(es_v, er_v, e_sem.at[0], e_sem.at[1], other)
    e_copy.start()

    load_k.wait()

    def scale_keys(i, _):
        rows = pl.ds(pl.multiple_of(i * SPAN, SPAN), SPAN)
        kd_v[rows, :] = (k_v[rows, :].astype(F32) * jnp.exp(total - run_v[rows, :])).astype(BF16)
        return 0

    lax.fori_loop(0, tok // SPAN, scale_keys, 0)
    load_v.wait()
    there = pl.ds(pl.multiple_of((1 - c) * half, half), half)
    here = pl.ds(pl.multiple_of(c * half, half), half)
    ss_v[1 - c] = mm_tn(v_v[:, there], kd_v[...]).astype(BF16)
    s_copy = remote(ss_v.at[1 - c], sr_v.at[1 - c], s_sem.at[0], s_sem.at[1], other)
    s_copy.start()
    own_v[...] = mm_tn(v_v[:, here], kd_v[...])
    ss_v[c] = own_v[...].astype(BF16)
    s2_copy = remote(ss_v.at[c], sr_v.at[c], s_sem.at[2], s_sem.at[3], other)
    s2_copy.start()

    e_copy.wait_recv()
    partner = er_v[0:1, :]
    first = jnp.where(c == 0, total, partner)
    second = jnp.where(c == 0, partner, total)
    lzs_v[...] = jnp.broadcast_to(total + partner, lzs_v.shape)
    lz_v[z] = lzs_v[...]
    lz_copies = []
    for d in far_first(nz):
        copy = remote(lzs_v, lz_v.at[z], lz_sem.at[0, d], lz_sem.at[1, d], {Z: (z + d) % nz})
        copy.start()
        lz_copies.append(copy)

    s_copy.wait_recv()
    decay = jnp.exp(second)
    one = jnp.ones_like(decay)
    mine = jnp.where(c == 0, decay, one)
    theirs = jnp.where(c == 0, one, decay)

    for j in range(nz):
        rows = slice(j * piece, (j + 1) * piece)
        zs_v[j] = (own_v[rows, :] * mine + sr_v[c, rows, :].astype(F32) * theirs).astype(BF16)
    zr_v[z] = zs_v[z]
    z_copies = {}
    for d in far_first(nz):
        j = (z + d) % nz
        copy = remote(zs_v.at[j], zr_v.at[z], z_sem.at[0, d], z_sem.at[1, d], {Z: j})
        copy.start()
        z_copies[d] = copy

    load_q.wait()
    early = jnp.where(c == 0, jnp.zeros_like(first), first)

    def scale_pair(i, _):
        rows = pl.ds(pl.multiple_of(i * SPAN, SPAN), SPAN)
        r = run_v[rows, :]
        mid = run_v[pl.ds(pl.multiple_of(i * SPAN + SPAN // 2, 8), 1), :]
        q = q_v[rows, :].astype(F32)
        k = k_v[rows, :].astype(F32)
        qa_v[rows, :] = (q * jnp.exp(r - mid)).astype(BF16)
        ka_v[rows, :] = (k * jnp.exp(mid - r)).astype(BF16)
        q0_v[rows, :] = (q * jnp.exp(r)).astype(BF16)
        qp_v[rows, :] = (q * jnp.exp(r + early)).astype(BF16)
        return 0

    lax.fori_loop(0, tok // SPAN, scale_pair, 0)

    for copy in lz_copies:
        copy.wait_recv()
    slab = lz_v[0]
    for j in range(1, nz):
        slab = slab + lz_v[j]
    lxs_v[...] = slab
    lx_v[x] = slab
    lx_copies = []
    for d in range(1, nx):
        copy = remote(lxs_v, lx_v.at[x], lx_sem.at[0, d], lx_sem.at[1, d], {X: (x + d) % nx})
        copy.start()
        lx_copies.append(copy)

    for h, ref in ((SPAN, b_v), (2 * SPAN, c_v), (4 * SPAN, d_v)):
        for start in range(0, tok, 2 * h):
            edge = run_v[start + h - 1:start + h, :]

            def scale_cross(i, _, start=start, h=h, ref=ref, edge=edge):
                ke = pl.ds(pl.multiple_of(start + i * SPAN, SPAN), SPAN)
                qe = pl.ds(pl.multiple_of(start + h + i * SPAN, SPAN), SPAN)
                ref[ke, :] = (k_v[ke, :].astype(F32) * jnp.exp(edge - run_v[ke, :])).astype(BF16)
                ref[qe, :] = (q_v[qe, :].astype(F32) * jnp.exp(run_v[qe, :] - edge)).astype(BF16)
                return 0

            lax.fori_loop(0, h // SPAN, scale_cross, 0)

    for d in near_first(nz):
        z_copies[d].wait_recv()
    run = jnp.zeros((piece, DK), F32)
    for j in range(nz):
        pre_v[j] = run
        run = run * jnp.exp(lz_v[j, 0:1, :]) + zr_v[j].astype(F32)
    xs_v[...] = run.astype(BF16)
    xr_v[x] = xs_v[...]
    x_copies = []
    for d in far_first(nx):
        copy = remote(xs_v, xr_v.at[x], x_sem.at[0, d], x_sem.at[1, d], {X: (x + d) % nx})
        copy.start()
        x_copies.append(copy)

    wide = 2 * SPAN
    ti = lax.broadcasted_iota(jnp.int32, (wide, wide), 0)
    si = lax.broadcasted_iota(jnp.int32, (wide, wide), 1)
    same = (ti // SPAN) == (si // SPAN)
    causal = same & (ti >= si)
    across = (ti // SPAN) > (si // SPAN)
    for m in range(tok // wide):
        rows = slice(m * wide, (m + 1) * wide)
        inside = mm_nt(qa_v[rows, :], ka_v[rows, :])
        between = mm_nt(b_v[rows, :], b_v[rows, :])
        diag = jnp.where(causal, inside, jnp.where(across, between, 0.0)).astype(BF16)
        if m % 2 == 0:
            wgt_v[rows, 0:wide] = diag
            wgt_v[rows, wide:2 * wide] = jnp.zeros_like(diag)
        else:
            before = slice((m - 1) * wide, m * wide)
            wgt_v[rows, 0:wide] = mm_nt(c_v[rows, :], c_v[before, :]).astype(BF16)
            wgt_v[rows, wide:2 * wide] = diag
    wd_v[...] = mm_nt(d_v[group:2 * group, :], d_v[0:group, :]).astype(BF16)
    s2_copy.wait_recv()
    for h in range(2):
        rows = slice(h * group, (h + 1) * group)
        acc = mm(wgt_v[rows, :], v_v[rows, :])
        if h:
            acc = acc + mm(wd_v[...], v_v[0:group, :])
        loc_v[rows, :] = acc

    keep = jnp.where(c == 0, 0.0, 1.0).astype(F32)
    for e in range(2):
        cols = slice(e * half, (e + 1) * half)
        state = (sr_v[e].astype(F32) * keep).astype(BF16)
        for h in range(2):
            rows = slice(h * group, (h + 1) * group)
            loc_v[rows, cols] = loc_v[rows, cols] + mm_nt(q0_v[rows, :], state)

    for copy in lx_copies:
        copy.wait_recv()
    for copy in x_copies:
        copy.wait_recv()
    enter = jnp.zeros((piece, DK), F32)
    for j in range(nx):
        nxt = enter * jnp.exp(lx_v[j, 0:1, :]) + xr_v[j].astype(F32)
        enter = jnp.where(j < x, nxt, enter)
    log = jnp.zeros((1, DK), F32)
    for j in range(nz):
        zb_v[j] = (pre_v[j] + enter * jnp.exp(log)).astype(BF16)
        log = log + lz_v[j, 0:1, :]
    inc_v[c, z] = zb_v[z]
    b_copies = {}
    for d in far_first(nz):
        j = (z + d) % nz
        copy = remote(zb_v.at[j], inc_v.at[c, z], b_sem.at[0, d], b_sem.at[1, d], {Z: j})
        copy.start()
        b_copies[d] = copy
    f_copies = []
    copy = remote(inc_v.at[c, z], inc_v.at[c, z], f_sem.at[0, 0], f_sem.at[1, 0], other)
    copy.start()
    f_copies.append(copy)

    load_og.wait()
    load_gain.wait()

    def gate_rows(i, _):
        rows = pl.ds(pl.multiple_of(i * SPAN, SPAN), SPAN)
        u = og_v[rows, :].astype(F32)
        gate_v[rows, :] = gain_v[...] * (u / (1.0 + jnp.exp(-u)))
        return 0

    lax.fori_loop(0, tok // SPAN, gate_rows, 0)
    load_w.wait()

    for d in near_first(nz):
        b_copies[d].wait_recv()
        owner = (z + nz - d) % nz
        copy = remote(inc_v.at[c, owner], inc_v.at[c, owner], f_sem.at[0, d], f_sem.at[1, d], other)
        copy.start()
        f_copies.append(copy)
    for copy in f_copies:
        copy.wait_recv()

    def columns(block):
        return pl.ds(pl.multiple_of(block * width, width), width)

    chunks = tok // SPAN
    order = []
    for i in range(chunks // 2):
        order += [(i, 0), (i + chunks // 2, 1)]
    p_copies = {}
    for ch, side in order:
        rows = slice(ch * SPAN, (ch + 1) * SPAN)
        near, far = (y_a, y_b) if side == 0 else (y_b, y_a)
        att = loc_v[rows, :] + mm_nt(qp_v[rows, :], inc_v[...].reshape(DV, DK))
        spread = jnp.mean(att * att, axis=-1, keepdims=True)
        gated = (att * lax.rsqrt(spread + 1e-05) * gate_v[rows, :]).astype(BF16)
        theirs_far = 3 - near if side == 0 else near + 1 - 2 * (near % 2)
        ps_v[ch, 0] = mm(gated, w_v[:, columns(near)]).astype(BF16)
        ps_v[ch, 1] = mm(gated, w_v[:, columns(theirs_far)]).astype(BF16)
        copy = remote(ps_v.at[ch], pr_v.at[ch], p_sem.at[0, ch], p_sem.at[1, ch], {Y: near})
        copy.start()
        p_copies[ch] = copy
        k0_v[ch] = mm(gated, w_v[:, columns(y)])
        k1_v[ch] = mm(gated, w_v[:, columns(far)])
    p2_copies = {}
    for ch, side in order:
        far = y_b if side == 0 else y_a
        p_copies[ch].wait_recv()
        p2s_v[ch] = (k1_v[ch] + pr_v[ch, 1].astype(F32)).astype(BF16)
        copy = remote(p2s_v.at[ch], p2r_v.at[ch], p2_sem.at[0, ch], p2_sem.at[1, ch], {Y: far})
        copy.start()
        p2_copies[ch] = copy
        k0_v[ch] = k0_v[ch] + pr_v[ch, 0].astype(F32)
    outs = []
    for ch, side in order:
        p2_copies[ch].wait_recv()
        o_v[ch] = (k0_v[ch] + p2r_v[ch].astype(F32)).astype(BF16)
        copy = pltpu.make_async_copy(
            o_v.at[ch], out_hbm.at[pl.ds(ch * SPAN, SPAN), :], out_sem.at[ch]
        )
        copy.start()
        outs.append(copy)

    sent = [e_copy, s_copy, s2_copy] + lz_copies + list(z_copies.values()) + lx_copies
    sent += x_copies + list(b_copies.values()) + f_copies
    sent += list(p_copies.values()) + list(p2_copies.values())
    for copy in sent:
        copy.wait_send()
    for copy in outs:
        copy.wait()


def shards(nx, nz, queries, key_vectors, values, log_gate, out_gate, norm_gain, out_weight):
    tok = queries.shape[0]
    width = out_weight.shape[1] // 4
    piece = DV // 2 // nz
    chunks = tok // SPAN
    any_spec = pl.BlockSpec(memory_space=pl.ANY)
    vmem, dma = pltpu.VMEM, pltpu.SemaphoreType.DMA
    row = (tok, DK)
    scratch = [
        vmem(row, BF16), vmem(row, BF16), vmem((tok, DV), BF16), vmem(row, BF16),
        vmem((tok, DV), BF16), vmem((1, DV), F32), vmem(out_weight.shape, BF16),
        vmem(row, F32), vmem(row, BF16), vmem(row, BF16), vmem(row, BF16), vmem(row, BF16),
        vmem(row, BF16), vmem(row, BF16), vmem(row, BF16), vmem(row, BF16),
        vmem((tok, 256), BF16), vmem((256, 256), BF16), vmem((tok, DV), F32), vmem((tok, DV), F32),
        vmem((8, DK), F32), vmem((8, DK), F32),
        vmem((2, DV // 2, DK), BF16), vmem((2, DV // 2, DK), BF16), vmem((DV // 2, DK), F32),
        vmem((8, DK), F32), vmem((nz, 8, DK), F32),
        vmem((nz, piece, DK), BF16), vmem((nz, piece, DK), BF16), vmem((nz, piece, DK), F32),
        vmem((8, DK), F32), vmem((nx, 8, DK), F32),
        vmem((piece, DK), BF16), vmem((nx, piece, DK), BF16),
        vmem((nz, piece, DK), BF16), vmem((2, nz, piece, DK), BF16),
        vmem((chunks, 2, SPAN, width), BF16), vmem((chunks, 2, SPAN, width), BF16),
        vmem((chunks, SPAN, width), F32), vmem((chunks, SPAN, width), F32),
        vmem((chunks, SPAN, width), BF16), vmem((chunks, SPAN, width), BF16),
        vmem((chunks, SPAN, width), BF16),
        dma((7,)), dma((chunks,)), dma((2,)), dma((4,)), dma((2, nz)), dma((2, nz)),
        dma((2, nx)), dma((2, nx)), dma((2, nz)), dma((2, nz)), dma((2, chunks)), dma((2, chunks)),
    ]
    return pl.pallas_call(
        functools.partial(body, nx, nz, tok, width),
        out_shape=jax.ShapeDtypeStruct((tok, width), BF16),
        in_specs=[any_spec] * 7,
        out_specs=any_spec,
        scratch_shapes=scratch,
        compiler_params=pltpu.CompilerParams(
            collective_id=0, has_side_effects=True, vmem_limit_bytes=48 * 2**20
        ),
    )(queries, key_vectors, values, log_gate, out_gate, norm_gain.reshape(1, DV), out_weight)


def build(devices, nx, nz):
    split = Mesh(devices.reshape(nx, nz, 2, 4), (X, Z, C, Y))
    in_specs = (P(SEQ, Y),) * 5 + (P(Y), P(Y, None))
    return jax.shard_map(
        functools.partial(shards, nx, nz),
        mesh=split, in_specs=in_specs, out_specs=P(SEQ, Y), check_vma=False,
    )


def solution(mesh):
    return build(mesh.devices, 4, mesh.shape["seq"] // 8)
```

time: 166 us -> 58.3 us (0.35)
  the two profiles are of different devices: /device:TPU:2 before, /device:TPU:1 now
where the time goes in v1:
time: 58.3 us; the launch traced here: 58 us
  Pallas kernels  49.9 us (86%)
  local copies, waits for them, and re-layouts  8 us (14%)
    pallas_call x1, Pallas kernels, shards(): pl.pallas_call(functools.partial(body, nx, nz, tok, width), out_shape=jax...  49.9 us
    unnamed x15, local copies, waits for them, and re-layouts  8 us

profile of v1, /device:TPU:1, one launch (start us, length us, event | category | flops | bytes accessed | tf_op | source)
XLA Modules:
  0.0 58.0 jit_solution(5303566619763513916)
XLA Ops:
  0.0 0.0 copy-start
  0.0 1.6 %copy-done = bf16[512,2048]{1,0:T(8,128)(2,1)S(1)} copy-done((bf16[512,2048]{1,0:T(8,128)(2,1)S(1)}, bf16[512,2048]{1,0:T(8,128)(2,1)}, u32[]{:S(2)}) %copy-start) | copy-done | bytes 2097176
  1.6 0.0 copy-start.1
  1.6 1.0 %copy-done.1 = bf16[512,512]{1,0:T(8,128)(2,1)S(1)} copy-done((bf16[512,512]{1,0:T(8,128)(2,1)S(1)}, bf16[512,512]{1,0:T(8,128)(2,1)}, u32[]{:S(2)}) %copy-start.1) | copy-done | bytes 524312
  2.6 0.0 copy-start.2
  2.6 1.0 %copy-done.2 = bf16[512,512]{1,0:T(8,128)(2,1)S(1)} copy-done((bf16[512,512]{1,0:T(8,128)(2,1)S(1)}, bf16[512,512]{1,0:T(8,128)(2,1)}, u32[]{:S(2)}) %copy-start.2) | copy-done | bytes 524312
  3.7 0.0 copy-start.3
  3.7 0.9 %copy-done.3 = bf16[512,256]{1,0:T(8,128)(2,1)S(1)} copy-done((bf16[512,256]{1,0:T(8,128)(2,1)S(1)}, bf16[512,256]{1,0:T(8,128)(2,1)}, u32[]{:S(2)}) %copy-start.3) | copy-done | bytes 262168
  4.6 0.0 copy-start.4
  4.6 0.9 %copy-done.4 = bf16[512,256]{1,0:T(8,128)(2,1)S(1)} copy-done((bf16[512,256]{1,0:T(8,128)(2,1)S(1)}, bf16[512,256]{1,0:T(8,128)(2,1)}, u32[]{:S(2)}) %copy-start.4) | copy-done | bytes 262168
  5.6 0.0 copy-start.5
  5.6 0.9 %copy-done.5 = bf16[512,256]{1,0:T(8,128)(2,1)S(1)} copy-done((bf16[512,256]{1,0:T(8,128)(2,1)S(1)}, bf16[512,256]{1,0:T(8,128)(2,1)}, u32[]{:S(2)}) %copy-start.5) | copy-done | bytes 262168
  6.5 0.0 copy-start.6
  6.5 0.7 %copy-done.6 = f32[512]{0:T(512)S(1)} copy-done((f32[512]{0:T(512)S(1)}, f32[512]{0:T(512)}, u32[]{:S(2)}) %copy-start.6) | copy-done | bytes 2072
  7.2 49.9 %shard_map.73 = bf16[512,512]{1,0:T(8,128)(2,1)S(1)} custom-call(bf16[512,256]{1,0:T(8,128)(2,1)S(1)} %copy-done.3, bf16[512,256]{1,0:T(8,128)(2,1)S(1)} %copy-done.4, bf16[512,512]{1,0:T(8,128)(2,1)S(1)} %copy-done.1, bf16[512,256]{1,0:T(8,128)(2,1)S(1)} %copy-done.5, bf16[512,512]{1,0:T(8,128)(2,1)S(1)} %copy-done.2, f32[1,512]{1,0:T(1,128)S(1)} %bitcast.1, ...), custom_call_target="tpu_custom_call" | custom-call | tf_op jit(solution)/shard_map/pallas_call | solution.py:364
  57.2 0.8 %copy.9 = bf16[512,512]{1,0:T(8,128)(2,1)} copy(bf16[512,512]{1,0:T(8,128)(2,1)S(1)} %shard_map.73) | data formatting | bytes 1048576
Async XLA Ops:
  0.0 1.6 %copy-start = (bf16[512,2048]{1,0:T(8,128)(2,1)S(1)}, bf16[512,2048]{1,0:T(8,128)(2,1)}, u32[]{:S(2)}) copy-start(bf16[512,2048]{1,0:T(8,128)(2,1)} %w_hbm.1) | copy-start | bytes 6291460
  1.6 1.0 %copy-start.1 = (bf16[512,512]{1,0:T(8,128)(2,1)S(1)}, bf16[512,512]{1,0:T(8,128)(2,1)}, u32[]{:S(2)}) copy-start(bf16[512,512]{1,0:T(8,128)(2,1)} %v_hbm.1) | copy-start | bytes 1572868
  2.6 1.0 %copy-start.2 = (bf16[512,512]{1,0:T(8,128)(2,1)S(1)}, bf16[512,512]{1,0:T(8,128)(2,1)}, u32[]{:S(2)}) copy-start(bf16[512,512]{1,0:T(8,128)(2,1)} %og_hbm.1) | copy-start | bytes 1572868
  3.7 0.9 %copy-start.3 = (bf16[512,256]{1,0:T(8,128)(2,1)S(1)}, bf16[512,256]{1,0:T(8,128)(2,1)}, u32[]{:S(2)}) copy-start(bf16[512,256]{1,0:T(8,128)(2,1)} %q_hbm.1) | copy-start | bytes 786436
  4.6 0.9 %copy-start.4 = (bf16[512,256]{1,0:T(8,128)(2,1)S(1)}, bf16[512,256]{1,0:T(8,128)(2,1)}, u32[]{:S(2)}) copy-start(bf16[512,256]{1,0:T(8,128)(2,1)} %k_hbm.1) | copy-start | bytes 786436
  5.6 0.9 %copy-start.5 = (bf16[512,256]{1,0:T(8,128)(2,1)S(1)}, bf16[512,256]{1,0:T(8,128)(2,1)}, u32[]{:S(2)}) copy-start(bf16[512,256]{1,0:T(8,128)(2,1)} %g_hbm.1) | copy-start | bytes 786436
  6.5 0.7 %copy-start.6 = (f32[512]{0:T(512)S(1)}, f32[512]{0:T(512)}, u32[]{:S(2)}) copy-start(f32[512]{0:T(512)} %param.12) | copy-start | bytes 6148

commit v2 on v1

v2 whole, which is shorter than its diff:
```python
import functools

import jax
import jax.numpy as jnp
from jax import lax
from jax.experimental import pallas as pl
from jax.experimental.pallas import tpu as pltpu
from jax.sharding import Mesh
from jax.sharding import PartitionSpec as P

DK = 256
DV = 512
SPAN = 64
X, Z, C, Y = ("seq_0", "seq_1", "seq_2", "head")
SEQ = (X, Z, C)
F32 = jnp.float32
BF16 = jnp.bfloat16
MESH_ID = pl.DeviceIdType.MESH
PROFILE = False


class Marks:
    def __init__(self):
        self.open = None

    def __call__(self, name):
        if not PROFILE:
            return
        if self.open is not None:
            self.open.__exit__(None, None, None)
        self.open = None
        if name:
            self.open = jax.named_scope(name)
            self.open.__enter__()


def mm(a, b):
    return lax.dot_general(a, b, (((1,), (0,)), ((), ())), preferred_element_type=F32)


def mm_nt(a, b):
    return lax.dot_general(a, b, (((1,), (1,)), ((), ())), preferred_element_type=F32)


def mm_tn(a, b):
    return lax.dot_general(a, b, (((0,), (0,)), ((), ())), preferred_element_type=F32)


def remote(src, dst, send, recv, where):
    return pltpu.make_async_remote_copy(
        src_ref=src, dst_ref=dst, send_sem=send, recv_sem=recv,
        device_id=where, device_id_type=MESH_ID,
    )


def far_first(n):
    return sorted(range(1, n), key=lambda d: (-min(d, n - d), d))


def near_first(n):
    return sorted(range(1, n), key=lambda d: (min(d, n - d), d))


def body(
    nx, nz, tok, width,
    q_hbm, k_hbm, v_hbm, g_hbm, og_hbm, gain_hbm, w_hbm, out_hbm,
    q_v, k_v, v_v, g_v, og_v, gain_v, w_v, wa_v, wb_v,
    run_v, kd_v, qa_v, ka_v, b_v, c_v, d_v, q0_v, qp_v, wgt_v, wd_v, loc_v, gate_v,
    es_v, er_v, ss_v, sr_v, own_v,
    lzs_v, lz_v, zs_v, zr_v, pre_v, lxs_v, lx_v, xs_v, xr_v, zb_v, inc_v,
    gs_v, gr_v, gm_v, rs_v, rr_v, k0_v, k1_v, fs_v, fr_v, o_v,
    in_sem, out_sem, e_sem, s_sem, lz_sem, z_sem, lx_sem, x_sem, b_sem, f_sem,
    wy_sem, wx_sem, wc_sem, wd_sem, g_sem, r_sem, n_sem,
):
    mark = Marks()
    x, z, c, y = (lax.axis_index(n) for n in (X, Z, C, Y))
    half = DV // 2
    piece = DV // nz
    y_a = y + 1 - 2 * (y % 2)
    y_b = 3 - y
    other = {C: 1 - c}
    z_to = [(z + d) % nz for d in range(nz)]
    z_from = [(z + nz - d) % nz for d in range(nz)]
    x_to = [(x + d) % nx for d in range(nx)]
    x_left = (x + nx - 1) % nx
    x_right = (x + 1) % nx

    e_copy = remote(es_v, er_v, e_sem.at[0], e_sem.at[1], other)
    s_copy = remote(ss_v, sr_v, s_sem.at[0], s_sem.at[1], other)
    lz_copies = {d: remote(lzs_v, lz_v.at[z], lz_sem.at[0, d], lz_sem.at[1, d], {Z: z_to[d]})
                 for d in range(1, nz)}
    z_copies = {d: remote(zs_v.at[z_to[d]], zr_v.at[z], z_sem.at[0, d], z_sem.at[1, d],
                          {Z: z_to[d]}) for d in range(1, nz)}
    lx_copies = {d: remote(lxs_v, lx_v.at[x], lx_sem.at[0, d], lx_sem.at[1, d], {X: x_to[d]})
                 for d in range(1, nx)}
    x_copies = {d: remote(xs_v, xr_v.at[x], x_sem.at[0, d], x_sem.at[1, d], {X: x_to[d]})
                for d in range(1, nx)}
    b_copies = {d: remote(zb_v.at[z_to[d]], inc_v.at[z], b_sem.at[0, d], b_sem.at[1, d],
                          {Z: z_to[d]}) for d in range(1, nz)}
    f_copies = {d: remote(inc_v.at[z_from[d]], inc_v.at[z_from[d]], f_sem.at[0, d],
                          f_sem.at[1, d], other) for d in range(nz)}

    parts = 8
    step = DV // 2 // parts

    def w_rows(parity, k):
        return pl.ds(pl.multiple_of(parity * (DV // 2) + k * step, step), step)

    near_half, far_half = x % 2, 1 - x % 2

    def wy(s, k):
        rows = w_rows(near_half, k)
        dst, to = ((wa_v, y_a), (wb_v, y_b))[s]
        return remote(w_v.at[rows, :], dst.at[rows, :], wy_sem.at[0, s, k], wy_sem.at[1, s, k],
                      {Y: to})

    def wx(s, k):
        rows = w_rows(near_half, k)
        buf, to = ((wa_v, x_left), (wb_v, x_right))[s]
        return remote(buf.at[rows, :], buf.at[rows, :], wx_sem.at[0, s, k], wx_sem.at[1, s, k],
                      {X: to})

    def wc(s, k):
        rows = w_rows(near_half, k)
        buf = (wa_v, wb_v)[s]
        return remote(buf.at[rows, :], buf.at[rows, :], wc_sem.at[0, s, k], wc_sem.at[1, s, k],
                      other)

    def wd(s, k):
        rows = w_rows(far_half, k)
        buf = (wa_v, wb_v)[s]
        return remote(buf.at[rows, :], buf.at[rows, :], wd_sem.at[0, s, k], wd_sem.at[1, s, k],
                      other)

    def pass_near(k):
        for s in range(2):
            wy(s, k).wait_recv()
            wx(s, k).start()
            wc(s, k).start()

    def pass_far(k):
        for s in range(2):
            wx(s, k).wait_recv()
            wd(s, k).start()

    def repeat(low, high, f):
        def one(k, _):
            f(k)
            return 0

        lax.fori_loop(low, high, one, 0)

    barrier = pltpu.get_barrier_semaphore()

    def greet(peers):
        for peer in peers:
            pl.semaphore_signal(barrier, inc=1, device_id=peer, device_id_type=MESH_ID)

    greet([other, {Y: y_a}, {Y: y_b}])

    @pl.when(c == 0)
    def _():
        greet([{X: x_left}, {X: x_right}])

    @pl.when(c == 1)
    def _():
        greet([{Z: z_to[d]} for d in range(1, nz)] + [{X: x_to[d]} for d in range(1, nx)])

    loads = []
    for i, (src, dst) in enumerate((
        (g_hbm, g_v), (k_hbm, k_v), (v_hbm, v_v), (w_hbm, w_v), (q_hbm, q_v),
        (og_hbm, og_v), (gain_hbm, gain_v),
    )):
        copy = pltpu.make_async_copy(src, dst, in_sem.at[i])
        copy.start()
        loads.append(copy)
    load_g, load_k, load_v, load_w, load_q, load_og, load_gain = loads

    group = 256
    tri = (
        lax.broadcasted_iota(jnp.int32, (group, group), 0)
        >= lax.broadcasted_iota(jnp.int32, (group, group), 1)
    ).astype(BF16)
    mark("w_g")
    load_g.wait()
    mark("cumsum")
    carry = jnp.zeros((1, DK), F32)
    for h in range(tok // group):
        rows = slice(h * group, (h + 1) * group)
        part = mm(tri, g_v[rows, :]) + carry
        run_v[rows, :] = part
        carry = part[group - 1:group, :]
    total = carry
    es_v[...] = total

    mark("keys")
    load_k.wait()

    def scale_keys(i):
        rows = pl.ds(pl.multiple_of(i * SPAN, SPAN), SPAN)
        kd_v[rows, :] = (k_v[rows, :].astype(F32) * jnp.exp(total - run_v[rows, :])).astype(BF16)

    repeat(0, tok // SPAN, scale_keys)
    mark("state")
    load_v.wait()
    for e in range(2):
        rows = slice(e * half, (e + 1) * half)
        own_v[rows, :] = mm_tn(v_v[:, rows], kd_v[...])
        ss_v[rows, :] = own_v[rows, :].astype(BF16)

    mark("w_barrier")

    @pl.when(c == 0)
    def _():
        pl.semaphore_wait(barrier, 5)
        e_copy.start()
        s_copy.start()
        load_w.wait()
        for k in range(parts):
            for s in range(2):
                wy(s, k).start()
        er_v[...] = jnp.zeros_like(er_v)

    @pl.when(c == 1)
    def _():
        pl.semaphore_wait(barrier, 3 + nz - 1 + nx - 1)

    mark("w_e")

    @pl.when(c == 1)
    def _():
        e_copy.wait_recv()
        lzs_v[...] = total + er_v[...]
        lz_v[z] = lzs_v[...]
        for d in far_first(nz):
            lz_copies[d].start()

    early = er_v[...]
    mark("w_s")

    @pl.when(c == 1)
    def _():
        s_copy.wait_recv()

    mark("chip_state")

    @pl.when(c == 1)
    def _():
        decay = jnp.exp(total)
        for j in range(nz):
            rows = slice(j * piece, (j + 1) * piece)
            zs_v[j] = (own_v[rows, :] + sr_v[rows, :].astype(F32) * decay).astype(BF16)
        for d in far_first(nz):
            z_copies[d].start()
        zr_v[z] = zs_v[z]
        load_w.wait()

    mark("scale_pair")
    load_q.wait()

    def scale_pair(i):
        rows = pl.ds(pl.multiple_of(i * SPAN, SPAN), SPAN)
        r = run_v[rows, :]
        mid = run_v[pl.ds(pl.multiple_of(i * SPAN + SPAN // 2, 8), 1), :]
        q = q_v[rows, :].astype(F32)
        k = k_v[rows, :].astype(F32)
        qa_v[rows, :] = (q * jnp.exp(r - mid)).astype(BF16)
        ka_v[rows, :] = (k * jnp.exp(mid - r)).astype(BF16)
        q0_v[rows, :] = (q * jnp.exp(r)).astype(BF16)
        qp_v[rows, :] = (q * jnp.exp(r + early)).astype(BF16)

    repeat(0, tok // SPAN, scale_pair)

    mark("scale_cross")
    for h, ref in ((SPAN, b_v), (2 * SPAN, c_v), (4 * SPAN, d_v)):
        for start in range(0, tok, 2 * h):
            edge = run_v[start + h - 1:start + h, :]

            def scale_cross(i, start=start, h=h, ref=ref, edge=edge):
                ke = pl.ds(pl.multiple_of(start + i * SPAN, SPAN), SPAN)
                qe = pl.ds(pl.multiple_of(start + h + i * SPAN, SPAN), SPAN)
                ref[ke, :] = (k_v[ke, :].astype(F32) * jnp.exp(edge - run_v[ke, :])).astype(BF16)
                ref[qe, :] = (q_v[qe, :].astype(F32) * jnp.exp(run_v[qe, :] - edge)).astype(BF16)

            repeat(0, h // SPAN, scale_cross)

    mark("attn")
    wide = 2 * SPAN
    ti = lax.broadcasted_iota(jnp.int32, (wide, wide), 0)
    si = lax.broadcasted_iota(jnp.int32, (wide, wide), 1)
    same = (ti // SPAN) == (si // SPAN)
    causal = same & (ti >= si)
    across = (ti // SPAN) > (si // SPAN)
    for m in range(tok // wide):
        rows = slice(m * wide, (m + 1) * wide)
        inside = mm_nt(qa_v[rows, :], ka_v[rows, :])
        between = mm_nt(b_v[rows, :], b_v[rows, :])
        diag = jnp.where(causal, inside, jnp.where(across, between, 0.0)).astype(BF16)
        if m % 2 == 0:
            wgt_v[rows, 0:wide] = diag
            wgt_v[rows, wide:2 * wide] = jnp.zeros_like(diag)
        else:
            before = slice((m - 1) * wide, m * wide)
            wgt_v[rows, 0:wide] = mm_nt(c_v[rows, :], c_v[before, :]).astype(BF16)
            wgt_v[rows, wide:2 * wide] = diag
    wd_v[...] = mm_nt(d_v[group:2 * group, :], d_v[0:group, :]).astype(BF16)
    for h in range(2):
        rows = slice(h * group, (h + 1) * group)
        acc = mm(wgt_v[rows, :], v_v[rows, :])
        if h:
            acc = acc + mm(wd_v[...], v_v[0:group, :])
        loc_v[rows, :] = acc

    @pl.when(c == 1)
    def _():
        for h in range(2):
            rows = slice(h * group, (h + 1) * group)
            loc_v[rows, :] = loc_v[rows, :] + mm_nt(q0_v[rows, :], sr_v[...])

    mark("gate")
    load_og.wait()
    load_gain.wait()

    def gate_rows(i):
        rows = pl.ds(pl.multiple_of(i * SPAN, SPAN), SPAN)
        u = og_v[rows, :].astype(F32)
        gate_v[rows, :] = gain_v[...] * (u / (1.0 + jnp.exp(-u)))

    repeat(0, tok // SPAN, gate_rows)

    mark("w_lz")

    @pl.when(c == 1)
    def _():
        for d in near_first(nz):
            lz_copies[d].wait_recv()
        slab = lz_v[0]
        for j in range(1, nz):
            slab = slab + lz_v[j]
        lxs_v[...] = slab
        lx_v[x] = slab
        for d in range(1, nx):
            lx_copies[d].start()

    mark("w_z")

    @pl.when(c == 1)
    def _():
        for d in near_first(nz):
            z_copies[d].wait_recv()

    mark("zprefix")

    @pl.when(c == 1)
    def _():
        run = jnp.zeros((piece, DK), F32)
        for j in range(nz):
            pre_v[j] = run
            run = run * jnp.exp(lz_v[j]) + zr_v[j].astype(F32)
        xs_v[...] = run.astype(BF16)
        for d in far_first(nx):
            x_copies[d].start()
        xr_v[x] = xs_v[...]

    mark("w_x")

    @pl.when(c == 1)
    def _():
        for d in range(1, nx):
            lx_copies[d].wait_recv()
        for d in near_first(nx):
            x_copies[d].wait_recv()

    mark("xprefix")

    @pl.when(c == 1)
    def _():
        enter = jnp.zeros((piece, DK), F32)
        for j in range(nx):
            nxt = enter * jnp.exp(lx_v[j]) + xr_v[j].astype(F32)
            enter = jnp.where(j < x, nxt, enter)
        log = jnp.zeros((1, DK), F32)
        for j in range(nz):
            zb_v[j] = (pre_v[j] + enter * jnp.exp(log)).astype(BF16)
            log = log + lz_v[j]
        for d in far_first(nz):
            b_copies[d].start()
        inc_v[z] = zb_v[z]
        f_copies[0].start()

    mark("w_b")

    @pl.when(c == 1)
    def _():
        for d in near_first(nz):
            b_copies[d].wait_recv()
            f_copies[d].start()

    mark("weights")
    ahead = 3

    @pl.when(c == 0)
    def _():
        def both(k):
            pass_near(k)
            pass_far(k - ahead)

        repeat(0, ahead, pass_near)
        repeat(ahead, parts, both)

    mark("w_f")

    @pl.when(c == 0)
    def _():
        for d in range(nz):
            f_copies[d].wait_recv()

    mark("gated")

    def columns(block):
        return pl.ds(pl.multiple_of(block * width, width), width)

    sides = (
        (y_a, y_b, y_b + 1 - 2 * (y_b % 2), ((y + 1) // 2) % 2, wa_v),
        (y_b, y_a, 3 - y_a, y // 2, wb_v),
    )
    side_tok = tok // 2
    chunks = side_tok // 2 // SPAN

    def start_row(s, own, j):
        lead = sides[s][3] if own else 1 - sides[s][3]
        return pl.multiple_of(s * side_tok + lead * (side_tok // 2) + j * SPAN, SPAN)

    def gated_rows(s, own, j):
        rows = pl.ds(start_row(s, own, j), SPAN)
        att = loc_v[rows, :] + mm_nt(qp_v[rows, :], inc_v[...].reshape(DV, DK))
        spread = jnp.mean(att * att, axis=-1, keepdims=True)
        return (att * lax.rsqrt(spread + 1e-05) * gate_v[rows, :]).astype(BF16)

    order = [(s, j) for j in range(chunks) for s in range(2)]
    g_copies, r_copies, n_copies = {}, {}, {}
    for s, j in order:
        gs_v[s, j] = gated_rows(s, False, j)
        g_copies[s, j] = remote(gs_v.at[s, j], gr_v.at[s, j], g_sem.at[0, s, j],
                                g_sem.at[1, s, j], {Y: sides[s][0]})
        g_copies[s, j].start()
    for s, j in order:
        gm_v[s, j] = gated_rows(s, True, j)

    mark("w_weights")

    @pl.when(c == 0)
    def _():
        repeat(parts - ahead, parts, pass_far)

    @pl.when(c == 1)
    def _():
        def arrive(k):
            for s in range(2):
                wc(s, k).wait_recv()
                wd(s, k).wait_recv()

        repeat(0, parts, arrive)

    mark("proj")

    def pair_sum(s, j, block):
        cols = columns(block)
        return mm(gm_v[s, j], w_v[:, cols]) + mm(gr_v[s, j], sides[s][4][:, cols])

    for s, j in order:
        near, far, far_near = sides[s][:3]
        g_copies[s, j].wait_recv()
        rs_v[s, j, 0] = pair_sum(s, j, far).astype(BF16)
        rs_v[s, j, 1] = pair_sum(s, j, far_near).astype(BF16)
        r_copies[s, j] = remote(rs_v.at[s, j], rr_v.at[s, j], r_sem.at[0, s, j],
                                r_sem.at[1, s, j], {Y: far})
        r_copies[s, j].start()
    mark("keep")
    for s, j in order:
        k1_v[s, j] = pair_sum(s, j, sides[s][0])
        k0_v[s, j] = pair_sum(s, j, y)
    mark("sum")
    outs = []

    def put(src, row, i):
        copy = pltpu.make_async_copy(src, out_hbm.at[pl.ds(row, SPAN), :], out_sem.at[i])
        copy.start()
        outs.append(copy)

    for s, j in order:
        r_copies[s, j].wait_recv()
        fs_v[s, j] = (k1_v[s, j] + rr_v[s, j, 1].astype(F32)).astype(BF16)
        n_copies[s, j] = remote(fs_v.at[s, j], fr_v.at[s, j], n_sem.at[0, s, j],
                                n_sem.at[1, s, j], {Y: sides[s][0]})
        n_copies[s, j].start()
        o_v[s, j] = (k0_v[s, j] + rr_v[s, j, 0].astype(F32)).astype(BF16)
        put(o_v.at[s, j], start_row(s, True, j), len(outs))
    mark("last")
    for s, j in order:
        n_copies[s, j].wait_recv()
        put(fr_v.at[s, j], start_row(s, False, j), len(outs))

    mark("drain")

    @pl.when(c == 0)
    def _():
        e_copy.wait_send()
        s_copy.wait_send()

        def sent(k):
            for s in range(2):
                for copy in (wy, wx, wc, wd):
                    copy(s, k).wait_send()

        repeat(0, parts, sent)

    @pl.when(c == 1)
    def _():
        for group_of in (lz_copies, z_copies, lx_copies, x_copies, b_copies, f_copies):
            for copy in group_of.values():
                copy.wait_send()

    for group_of in (g_copies, r_copies, n_copies):
        for copy in group_of.values():
            copy.wait_send()
    for copy in outs:
        copy.wait()
    mark(None)


def shards(nx, nz, queries, key_vectors, values, log_gate, out_gate, norm_gain, out_weight):
    tok = queries.shape[0]
    width = out_weight.shape[1] // 4
    piece = DV // nz
    chunks = tok // 4 // SPAN
    any_spec = pl.BlockSpec(memory_space=pl.ANY)
    vmem, dma = pltpu.VMEM, pltpu.SemaphoreType.DMA
    row = (tok, DK)
    weights = vmem(out_weight.shape, BF16)
    blocks = (2, chunks, SPAN, width)
    scratch = [
        vmem(row, BF16), vmem(row, BF16), vmem((tok, DV), BF16), vmem(row, BF16),
        vmem((tok, DV), BF16), vmem((1, DV), F32), weights, weights, weights,
        vmem(row, F32), vmem(row, BF16), vmem(row, BF16), vmem(row, BF16), vmem(row, BF16),
        vmem(row, BF16), vmem(row, BF16), vmem(row, BF16), vmem(row, BF16),
        vmem((tok, 256), BF16), vmem((256, 256), BF16), vmem((tok, DV), F32), vmem((tok, DV), F32),
        vmem((1, DK), F32), vmem((1, DK), F32),
        vmem((DV, DK), BF16), vmem((DV, DK), BF16), vmem((DV, DK), F32),
        vmem((1, DK), F32), vmem((nz, 1, DK), F32),
        vmem((nz, piece, DK), BF16), vmem((nz, piece, DK), BF16), vmem((nz, piece, DK), F32),
        vmem((1, DK), F32), vmem((nx, 1, DK), F32),
        vmem((piece, DK), BF16), vmem((nx, piece, DK), BF16),
        vmem((nz, piece, DK), BF16), vmem((nz, piece, DK), BF16),
        vmem(blocks, BF16), vmem(blocks, BF16), vmem(blocks, BF16),
        vmem((2, chunks, 2, SPAN, width), BF16), vmem((2, chunks, 2, SPAN, width), BF16),
        vmem(blocks, F32), vmem(blocks, F32),
        vmem(blocks, BF16), vmem(blocks, BF16), vmem(blocks, BF16),
        dma((7,)), dma((4 * chunks,)), dma((2,)), dma((2,)), dma((2, nz)), dma((2, nz)),
        dma((2, nx)), dma((2, nx)), dma((2, nz)), dma((2, nz)),
        dma((2, 2, 8)), dma((2, 2, 8)), dma((2, 2, 8)), dma((2, 2, 8)),
        dma((2, 2, chunks)), dma((2, 2, chunks)), dma((2, 2, chunks)),
    ]
    return pl.pallas_call(
        functools.partial(body, nx, nz, tok, width),
        out_shape=jax.ShapeDtypeStruct((tok, width), BF16),
        in_specs=[any_spec] * 7,
        out_specs=any_spec,
        scratch_shapes=scratch,
        compiler_params=pltpu.CompilerParams(
            collective_id=0, has_side_effects=True, vmem_limit_bytes=67043328
        ),
    )(queries, key_vectors, values, log_gate, out_gate, norm_gain.reshape(1, DV), out_weight)


def build(devices, nx, nz):
    split = Mesh(devices.reshape(nx, nz, 2, 4), (X, Z, C, Y))
    in_specs = (P(SEQ, Y),) * 5 + (P(Y), P(Y, None))
    return jax.shard_map(
        functools.partial(shards, nx, nz),
        mesh=split, in_specs=in_specs, out_specs=P(SEQ, Y), check_vma=False,
    )


def solution(mesh):
    return build(mesh.devices, 4, mesh.shape["seq"] // 8)
```

time: 58.3 us -> 45.6 us (0.78)
  the two profiles are of different devices: /device:TPU:1 before, /device:TPU:2 now
where the time goes in v2:
time: 45.6 us; the launch traced here: 45.2 us
  Pallas kernels  43.4 us (95%)
  local copies, waits for them, and re-layouts  1.87 us (4%)
    pallas_call x1, Pallas kernels, shards(): pl.pallas_call(functools.partial(body, nx, nz, tok, width), out_shape=jax...  43.4 us
    unnamed x1, local copies, waits for them, and re-layouts  1.87 us

profile of v2, /device:TPU:2, one launch (start us, length us, event | category | flops | bytes accessed | tf_op | source)
XLA Modules:
  0.0 45.2 jit_solution(2516611277090553530)
XLA Ops:
  0.0 43.4 %shard_map.73 = bf16[512,512]{1,0:T(8,128)(2,1)} custom-call(bf16[512,256]{1,0:T(8,128)(2,1)} %q_hbm.1, bf16[512,256]{1,0:T(8,128)(2,1)} %k_hbm.1, bf16[512,512]{1,0:T(8,128)(2,1)} %v_hbm.1, bf16[512,256]{1,0:T(8,128)(2,1)} %g_hbm.1, bf16[512,512]{1,0:T(8,128)(2,1)} %og_hbm.1, f32[1,512]{1,0:T(1,128)} %bitcast.1, bf16[512,2048]{1,0:T(8,128)(2,1)} %w_hbm.1), custom_call_target="tpu_custom_call" | custom-call | tf_op jit(solution)/shard_map/pallas_call | solution.py:564
  43.4 1.9 %copy.9 = bf16[512,512]{1,0:T(8,128)(2,1)} copy(bf16[512,512]{1,0:T(8,128)(2,1)} %shard_map.73) | data formatting | bytes 1048576

commit v3 on v2

--- a/solution.py
+++ b/solution.py
@@ -64,13 +64,13 @@
 def body(
     nx, nz, tok, width,
     q_hbm, k_hbm, v_hbm, g_hbm, og_hbm, gain_hbm, w_hbm, out_hbm,
-    q_v, k_v, v_v, g_v, og_v, gain_v, w_v, wa_v, wb_v,
+    q_v, k_v, v_v, g_v, og_v, gain_v, w_v, wn_v,
     run_v, kd_v, qa_v, ka_v, b_v, c_v, d_v, q0_v, qp_v, wgt_v, wd_v, loc_v, gate_v,
     es_v, er_v, ss_v, sr_v, own_v,
-    lzs_v, lz_v, zs_v, zr_v, pre_v, lxs_v, lx_v, xs_v, xr_v, zb_v, inc_v,
+    lzs_v, lz_v, zs_v, zr_v, pre_v, lxs_v, lx_v, xs_v, xr_v, ent_v, zb_v, inc_v,
     gs_v, gr_v, gm_v, rs_v, rr_v, k0_v, k1_v, fs_v, fr_v, o_v,
     in_sem, out_sem, e_sem, s_sem, lz_sem, z_sem, lx_sem, x_sem, b_sem, f_sem,
-    wy_sem, wx_sem, wc_sem, wd_sem, g_sem, r_sem, n_sem,
+    wy_sem, wx_sem, wc_sem, g_sem, r_sem, n_sem,
 ):
     mark = Marks()
     x, z, c, y = (lax.axis_index(n) for n in (X, Z, C, Y))
@@ -87,60 +87,79 @@
 
     e_copy = remote(es_v, er_v, e_sem.at[0], e_sem.at[1], other)
     s_copy = remote(ss_v, sr_v, s_sem.at[0], s_sem.at[1], other)
-    lz_copies = {d: remote(lzs_v, lz_v.at[z], lz_sem.at[0, d], lz_sem.at[1, d], {Z: z_to[d]})
+    most = pl.ds(0, nz - 1)
+    lz_copies = {d: remote(lzs_v, lz_v.at[z], lz_sem.at[0], lz_sem.at[1], {Z: z_to[d]})
                  for d in range(1, nz)}
-    z_copies = {d: remote(zs_v.at[z_to[d]], zr_v.at[z], z_sem.at[0, d], z_sem.at[1, d],
+    lz_all = remote(lz_v.at[most], lz_v.at[most], lz_sem.at[0], lz_sem.at[1], other)
+    z_copies = {d: remote(zs_v.at[z_to[d]], zr_v.at[z], z_sem.at[0], z_sem.at[1],
                           {Z: z_to[d]}) for d in range(1, nz)}
-    lx_copies = {d: remote(lxs_v, lx_v.at[x], lx_sem.at[0, d], lx_sem.at[1, d], {X: x_to[d]})
-                 for d in range(1, nx)}
-    x_copies = {d: remote(xs_v, xr_v.at[x], x_sem.at[0, d], x_sem.at[1, d], {X: x_to[d]})
-                for d in range(1, nx)}
-    b_copies = {d: remote(zb_v.at[z_to[d]], inc_v.at[z], b_sem.at[0, d], b_sem.at[1, d],
+    z_all = remote(zs_v.at[most], zr_v.at[most], z_sem.at[0], z_sem.at[1], other)
+    lx_copies = {d: remote(lxs_v, lx_v.at[x], lx_sem.at[0, d - 1], lx_sem.at[1, d - 1],
+                           {X: x_to[d]}) for d in range(1, nx)}
+    x_copies = {d: remote(xs_v, xr_v.at[x], x_sem.at[0, d - 1], x_sem.at[1, d - 1],
+                          {X: x_to[d]}) for d in range(1, nx)}
+    b_copies = {d: remote(zb_v.at[z_to[d]], inc_v.at[z], b_sem.at[0], b_sem.at[d],
                           {Z: z_to[d]}) for d in range(1, nz)}
-    f_copies = {d: remote(inc_v.at[z_from[d]], inc_v.at[z_from[d]], f_sem.at[0, d],
-                          f_sem.at[1, d], other) for d in range(nz)}
-
-    parts = 8
-    step = DV // 2 // parts
-
-    def w_rows(parity, k):
-        return pl.ds(pl.multiple_of(parity * (DV // 2) + k * step, step), step)
+    b_all = remote(zb_v.at[most], inc_v.at[most], b_sem.at[0], b_sem.at[1], other)
+    f_copies = {d: remote(inc_v.at[z_from[d]], inc_v.at[z_from[d]], f_sem.at[0],
+                          f_sem.at[1], other) for d in range(nz)}
+    f_all = remote(inc_v, inc_v, f_sem.at[0], f_sem.at[1], other)
+
+    def step_a(v):
+        return v + 1 - 2 * (v % 2)
+
+    def near_of(s, v):
+        return jnp.where(s == 0, step_a(v), 3 - v)
+
+    def far_of(s, v):
+        return jnp.where(s == 0, 3 - v, step_a(v))
+
+    def columns(block):
+        return pl.ds(pl.multiple_of(block * width, width), width)
+
+    parts = 4
+    step = DV // 2
+
+    def w_part(s, owner, parity, k):
+        far = far_of(s, owner)
+        block = (far, near_of(s, far), near_of(s, owner), owner)[k]
+        return pl.ds(pl.multiple_of(parity * step, step), step), columns(block)
 
     near_half, far_half = x % 2, 1 - x % 2
 
     def wy(s, k):
-        rows = w_rows(near_half, k)
-        dst, to = ((wa_v, y_a), (wb_v, y_b))[s]
-        return remote(w_v.at[rows, :], dst.at[rows, :], wy_sem.at[0, s, k], wy_sem.at[1, s, k],
+        to = near_of(s, y)
+        rows, cols = w_part(s, to, near_half, k)
+        return remote(w_v.at[rows, cols], wn_v.at[s, rows, cols], wy_sem.at[0], wy_sem.at[1 + k],
                       {Y: to})
 
+    def passed(s, k, parity, send, recv, to):
+        rows, cols = w_part(s, y, parity, k)
+        buf = wn_v.at[s, rows, cols]
+        return remote(buf, buf, send, recv, to)
+
     def wx(s, k):
-        rows = w_rows(near_half, k)
-        buf, to = ((wa_v, x_left), (wb_v, x_right))[s]
-        return remote(buf.at[rows, :], buf.at[rows, :], wx_sem.at[0, s, k], wx_sem.at[1, s, k],
-                      {X: to})
+        return passed(s, k, near_half, wx_sem.at[0], wx_sem.at[1 + k], {X: (x_left, x_right)[s]})
 
     def wc(s, k):
-        rows = w_rows(near_half, k)
-        buf = (wa_v, wb_v)[s]
-        return remote(buf.at[rows, :], buf.at[rows, :], wc_sem.at[0, s, k], wc_sem.at[1, s, k],
-                      other)
+        return passed(s, k, near_half, wc_sem.at[0], wc_sem.at[1 + k // 2], other)
 
     def wd(s, k):
-        rows = w_rows(far_half, k)
-        buf = (wa_v, wb_v)[s]
-        return remote(buf.at[rows, :], buf.at[rows, :], wd_sem.at[0, s, k], wd_sem.at[1, s, k],
-                      other)
+        return passed(s, k, far_half, wc_sem.at[0], wc_sem.at[1 + k // 2], other)
+
+    def part_wait(sem, k):
+        two = wn_v.at[:, pl.ds(0, step), pl.ds(0, width)]
+        remote(two, two, sem.at[0], sem.at[1 + k], other).wait_recv()
 
     def pass_near(k):
+        part_wait(wy_sem, k)
         for s in range(2):
-            wy(s, k).wait_recv()
             wx(s, k).start()
             wc(s, k).start()
 
     def pass_far(k):
+        part_wait(wx_sem, k)
         for s in range(2):
-            wx(s, k).wait_recv()
             wd(s, k).start()
 
     def repeat(low, high, f):
@@ -332,22 +351,19 @@
 
     @pl.when(c == 1)
     def _():
-        for d in near_first(nz):
-            lz_copies[d].wait_recv()
+        lz_all.wait_recv()
         slab = lz_v[0]
         for j in range(1, nz):
             slab = slab + lz_v[j]
         lxs_v[...] = slab
-        lx_v[x] = slab
         for d in range(1, nx):
-            lx_copies[d].start()
+            pl.when(x + d < nx)(lx_copies[d].start)
 
     mark("w_z")
 
     @pl.when(c == 1)
     def _():
-        for d in near_first(nz):
-            z_copies[d].wait_recv()
+        z_all.wait_recv()
 
     mark("zprefix")
 
@@ -359,26 +375,27 @@
             run = run * jnp.exp(lz_v[j]) + zr_v[j].astype(F32)
         xs_v[...] = run.astype(BF16)
         for d in far_first(nx):
-            x_copies[d].start()
-        xr_v[x] = xs_v[...]
+            pl.when(x + d < nx)(x_copies[d].start)
 
     mark("w_x")
 
     @pl.when(c == 1)
     def _():
         for d in range(1, nx):
-            lx_copies[d].wait_recv()
+            pl.when(x >= d)(lx_copies[d].wait_recv)
         for d in near_first(nx):
-            x_copies[d].wait_recv()
+            pl.when(x >= d)(x_copies[d].wait_recv)
 
     mark("xprefix")
 
     @pl.when(c == 1)
     def _():
-        enter = jnp.zeros((piece, DK), F32)
-        for j in range(nx):
-            nxt = enter * jnp.exp(lx_v[j]) + xr_v[j].astype(F32)
-            enter = jnp.where(j < x, nxt, enter)
+        ent_v[...] = jnp.zeros_like(ent_v)
+        for j in range(nx - 1):
+            @pl.when(j < x)
+            def _(j=j):
+                ent_v[...] = ent_v[...] * jnp.exp(lx_v[j]) + xr_v[j].astype(F32)
+        enter = ent_v[...]
         log = jnp.zeros((1, DK), F32)
         for j in range(nz):
             zb_v[j] = (pre_v[j] + enter * jnp.exp(log)).astype(BF16)
@@ -397,38 +414,29 @@
             f_copies[d].start()
 
     mark("weights")
-    ahead = 3
+    ahead = 2
 
     @pl.when(c == 0)
     def _():
-        def both(k):
+        for k in range(parts):
             pass_near(k)
-            pass_far(k - ahead)
-
-        repeat(0, ahead, pass_near)
-        repeat(ahead, parts, both)
+            if k >= ahead:
+                pass_far(k - ahead)
 
     mark("w_f")
 
     @pl.when(c == 0)
     def _():
-        for d in range(nz):
-            f_copies[d].wait_recv()
+        f_all.wait_recv()
 
     mark("gated")
-
-    def columns(block):
-        return pl.ds(pl.multiple_of(block * width, width), width)
-
-    sides = (
-        (y_a, y_b, y_b + 1 - 2 * (y_b % 2), ((y + 1) // 2) % 2, wa_v),
-        (y_b, y_a, 3 - y_a, y // 2, wb_v),
-    )
     side_tok = tok // 2
     chunks = side_tok // 2 // SPAN
+    order = [(s, j) for j in range(chunks) for s in (0, 1)]
 
     def start_row(s, own, j):
-        lead = sides[s][3] if own else 1 - sides[s][3]
+        lead = jnp.where(s == 0, ((y + 1) // 2) % 2, y // 2)
+        lead = lead if own else 1 - lead
         return pl.multiple_of(s * side_tok + lead * (side_tok // 2) + j * SPAN, SPAN)
 
     def gated_rows(s, own, j):
@@ -437,69 +445,78 @@
         spread = jnp.mean(att * att, axis=-1, keepdims=True)
         return (att * lax.rsqrt(spread + 1e-05) * gate_v[rows, :]).astype(BF16)
 
-    order = [(s, j) for j in range(chunks) for s in range(2)]
-    g_copies, r_copies, n_copies = {}, {}, {}
+    g_copies, r_copies, n_copies = [], [], []
     for s, j in order:
         gs_v[s, j] = gated_rows(s, False, j)
-        g_copies[s, j] = remote(gs_v.at[s, j], gr_v.at[s, j], g_sem.at[0, s, j],
-                                g_sem.at[1, s, j], {Y: sides[s][0]})
-        g_copies[s, j].start()
+        g_copies.append(remote(gs_v.at[s, j], gr_v.at[s, j], g_sem.at[chunks * 2],
+                               g_sem.at[s * chunks + j], {Y: near_of(s, y)}))
+        g_copies[-1].start()
+        r_copies.append(remote(rs_v.at[s, j], rr_v.at[s, j], r_sem.at[chunks * 2],
+                               r_sem.at[s * chunks + j], {Y: far_of(s, y)}))
+        n_copies.append(remote(fs_v.at[s, j], fr_v.at[s, j], n_sem.at[chunks * 2],
+                               n_sem.at[s * chunks + j], {Y: near_of(s, y)}))
     for s, j in order:
         gm_v[s, j] = gated_rows(s, True, j)
 
     mark("w_weights")
 
-    @pl.when(c == 0)
-    def _():
-        repeat(parts - ahead, parts, pass_far)
-
-    @pl.when(c == 1)
-    def _():
-        def arrive(k):
-            for s in range(2):
-                wc(s, k).wait_recv()
-                wd(s, k).wait_recv()
-
-        repeat(0, parts, arrive)
+    def arrive(i):
+        both = wn_v.at[0]
+        remote(both, both, wc_sem.at[0], wc_sem.at[1 + i], other).wait_recv()
+
+    @pl.when(c == 1)
+    def _():
+        arrive(0)
 
     mark("proj")
 
     def pair_sum(s, j, block):
         cols = columns(block)
-        return mm(gm_v[s, j], w_v[:, cols]) + mm(gr_v[s, j], sides[s][4][:, cols])
-
-    for s, j in order:
-        near, far, far_near = sides[s][:3]
-        g_copies[s, j].wait_recv()
+        return mm(gm_v[s, j], w_v[:, cols]) + mm(gr_v[s, j], wn_v[s, :, cols])
+
+    for i, (s, j) in enumerate(order):
+        far = far_of(s, y)
+        mark(f"w_gather{i}")
+        g_copies[i].wait_recv()
+        mark(f"proj{i}")
         rs_v[s, j, 0] = pair_sum(s, j, far).astype(BF16)
-        rs_v[s, j, 1] = pair_sum(s, j, far_near).astype(BF16)
-        r_copies[s, j] = remote(rs_v.at[s, j], rr_v.at[s, j], r_sem.at[0, s, j],
-                                r_sem.at[1, s, j], {Y: far})
-        r_copies[s, j].start()
+        rs_v[s, j, 1] = pair_sum(s, j, near_of(s, far)).astype(BF16)
+        r_copies[i].start()
+        if i < ahead:
+            mark(f"w_far{i}")
+
+            @pl.when(c == 0)
+            def _(i=i):
+                pass_far(parts - ahead + i)
+
+    mark("w_weights2")
+
+    @pl.when(c == 1)
+    def _():
+        arrive(1)
+
     mark("keep")
     for s, j in order:
-        k1_v[s, j] = pair_sum(s, j, sides[s][0])
+        k1_v[s, j] = pair_sum(s, j, near_of(s, y))
         k0_v[s, j] = pair_sum(s, j, y)
     mark("sum")
-    outs = []
-
-    def put(src, row, i):
-        copy = pltpu.make_async_copy(src, out_hbm.at[pl.ds(row, SPAN), :], out_sem.at[i])
-        copy.start()
-        outs.append(copy)
-
-    for s, j in order:
-        r_copies[s, j].wait_recv()
+
+    def put(src, row):
+        pltpu.make_async_copy(src, out_hbm.at[pl.ds(row, SPAN), :], out_sem.at[0]).start()
+
+    for i, (s, j) in enumerate(order):
+        mark(f"w_r{i}")
+        r_copies[i].wait_recv()
+        mark(f"sum{i}")
         fs_v[s, j] = (k1_v[s, j] + rr_v[s, j, 1].astype(F32)).astype(BF16)
-        n_copies[s, j] = remote(fs_v.at[s, j], fr_v.at[s, j], n_sem.at[0, s, j],
-                                n_sem.at[1, s, j], {Y: sides[s][0]})
-        n_copies[s, j].start()
+        n_copies[i].start()
         o_v[s, j] = (k0_v[s, j] + rr_v[s, j, 0].astype(F32)).astype(BF16)
-        put(o_v.at[s, j], start_row(s, True, j), len(outs))
+        put(o_v.at[s, j], start_row(s, True, j))
     mark("last")
-    for s, j in order:
-        n_copies[s, j].wait_recv()
-        put(fr_v.at[s, j], start_row(s, False, j), len(outs))
+    for i, (s, j) in enumerate(order):
+        mark(f"w_n{i}")
+        n_copies[i].wait_recv()
+        put(fr_v.at[s, j], start_row(s, False, j))
 
     mark("drain")
 
@@ -508,24 +525,22 @@
         e_copy.wait_send()
         s_copy.wait_send()
 
-        def sent(k):
-            for s in range(2):
-                for copy in (wy, wx, wc, wd):
-                    copy(s, k).wait_send()
-
-        repeat(0, parts, sent)
-
-    @pl.when(c == 1)
-    def _():
-        for group_of in (lz_copies, z_copies, lx_copies, x_copies, b_copies, f_copies):
-            for copy in group_of.values():
-                copy.wait_send()
-
-    for group_of in (g_copies, r_copies, n_copies):
-        for copy in group_of.values():
+        one = wn_v.at[0]
+        for sem in (wy_sem, wx_sem):
+            remote(one, one, sem.at[0], sem.at[1], other).wait_send()
+        remote(wn_v, wn_v, wc_sem.at[0], wc_sem.at[1], other).wait_send()
+
+    @pl.when(c == 1)
+    def _():
+        for copy in (lz_all, z_all, b_all, f_all):
             copy.wait_send()
-    for copy in outs:
-        copy.wait()
+        for d in range(1, nx):
+            pl.when(x + d < nx)(lx_copies[d].wait_send)
+            pl.when(x + d < nx)(x_copies[d].wait_send)
+
+    for buf, sem in ((gs_v, g_sem), (rs_v, r_sem), (fs_v, n_sem)):
+        remote(buf, buf, sem.at[chunks * 2], sem.at[0], other).wait_send()
+    pltpu.make_async_copy(v_v, out_hbm, out_sem.at[0]).wait()
     mark(None)
 
 
@@ -541,7 +556,7 @@
     blocks = (2, chunks, SPAN, width)
     scratch = [
         vmem(row, BF16), vmem(row, BF16), vmem((tok, DV), BF16), vmem(row, BF16),
-        vmem((tok, DV), BF16), vmem((1, DV), F32), weights, weights, weights,
+        vmem((tok, DV), BF16), vmem((1, DV), F32), weights, vmem((2,) + out_weight.shape, BF16),
         vmem(row, F32), vmem(row, BF16), vmem(row, BF16), vmem(row, BF16), vmem(row, BF16),
         vmem(row, BF16), vmem(row, BF16), vmem(row, BF16), vmem(row, BF16),
         vmem((tok, 256), BF16), vmem((256, 256), BF16), vmem((tok, DV), F32), vmem((tok, DV), F32),
@@ -550,16 +565,16 @@
         vmem((1, DK), F32), vmem((nz, 1, DK), F32),
         vmem((nz, piece, DK), BF16), vmem((nz, piece, DK), BF16), vmem((nz, piece, DK), F32),
         vmem((1, DK), F32), vmem((nx, 1, DK), F32),
-        vmem((piece, DK), BF16), vmem((nx, piece, DK), BF16),
+        vmem((piece, DK), BF16), vmem((nx, piece, DK), BF16), vmem((piece, DK), F32),
         vmem((nz, piece, DK), BF16), vmem((nz, piece, DK), BF16),
         vmem(blocks, BF16), vmem(blocks, BF16), vmem(blocks, BF16),
         vmem((2, chunks, 2, SPAN, width), BF16), vmem((2, chunks, 2, SPAN, width), BF16),
         vmem(blocks, F32), vmem(blocks, F32),
         vmem(blocks, BF16), vmem(blocks, BF16), vmem(blocks, BF16),
-        dma((7,)), dma((4 * chunks,)), dma((2,)), dma((2,)), dma((2, nz)), dma((2, nz)),
-        dma((2, nx)), dma((2, nx)), dma((2, nz)), dma((2, nz)),
-        dma((2, 2, 8)), dma((2, 2, 8)), dma((2, 2, 8)), dma((2, 2, 8)),
-        dma((2, 2, chunks)), dma((2, 2, chunks)), dma((2, 2, chunks)),
+        dma((7,)), dma((1,)), dma((2,)), dma((2,)), dma((2,)), dma((2,)),
+        dma((2, nx - 1)), dma((2, nx - 1)), dma((nz,)), dma((2,)),
+        dma((5,)), dma((5,)), dma((3,)),
+        dma((2 * chunks + 1,)), dma((2 * chunks + 1,)), dma((2 * chunks + 1,)),
     ]
     return pl.pallas_call(
         functools.partial(body, nx, nz, tok, width),

time: 45.6 us -> 41.4 us (0.908)
  Pallas kernels: 43.4 us -> 39.4 us
    pallas_call x1, Pallas kernels: 43.4 us -> 39.4 us  [shards(): pl.pallas_call(functools.partial(body, nx, nz, tok, width), out_shape=jax...]
where the time goes in v3:
time: 41.4 us; the launch traced here: 41.3 us
  Pallas kernels  39.4 us (95%)
  local copies, waits for them, and re-layouts  1.87 us (5%)
    pallas_call x1, Pallas kernels, shards(): pl.pallas_call(functools.partial(body, nx, nz, tok, width), out_shape=jax...  39.4 us
    unnamed x1, local copies, waits for them, and re-layouts  1.87 us

profile of v3, /device:TPU:2, one launch (start us, length us, event | category | flops | bytes accessed | tf_op | source)
XLA Modules:
  0.0 41.3 jit_solution(16632202924858449477)
XLA Ops:
  0.0 39.4 %shard_map.73 = bf16[512,512]{1,0:T(8,128)(2,1)} custom-call(bf16[512,256]{1,0:T(8,128)(2,1)} %q_hbm.1, bf16[512,256]{1,0:T(8,128)(2,1)} %k_hbm.1, bf16[512,512]{1,0:T(8,128)(2,1)} %v_hbm.1, bf16[512,256]{1,0:T(8,128)(2,1)} %g_hbm.1, bf16[512,512]{1,0:T(8,128)(2,1)} %og_hbm.1, f32[1,512]{1,0:T(1,128)} %bitcast.1, bf16[512,2048]{1,0:T(8,128)(2,1)} %w_hbm.1), custom_call_target="tpu_custom_call" | custom-call | tf_op jit(solution)/shard_map/pallas_call | solution.py:579
  39.4 1.9 %copy.9 = bf16[512,512]{1,0:T(8,128)(2,1)} copy(bf16[512,512]{1,0:T(8,128)(2,1)} %shard_map.73) | data formatting | bytes 1048576

commit v4 on v3

--- a/solution.py
+++ b/solution.py
@@ -63,13 +63,13 @@
 
 def body(
     nx, nz, tok, width,
-    q_hbm, k_hbm, v_hbm, g_hbm, og_hbm, gain_hbm, w_hbm, out_hbm,
+    q_hbm, k_hbm, v_hbm, g_hbm, og_hbm, gain_hbm, w_hbm, out_ref,
     q_v, k_v, v_v, g_v, og_v, gain_v, w_v, wn_v,
     run_v, kd_v, qa_v, ka_v, b_v, c_v, d_v, q0_v, qp_v, wgt_v, wd_v, loc_v, gate_v,
     es_v, er_v, ss_v, sr_v, own_v,
     lzs_v, lz_v, zs_v, zr_v, pre_v, lxs_v, lx_v, xs_v, xr_v, ent_v, zb_v, inc_v,
-    gs_v, gr_v, gm_v, rs_v, rr_v, k0_v, k1_v, fs_v, fr_v, o_v,
-    in_sem, out_sem, e_sem, s_sem, lz_sem, z_sem, lx_sem, x_sem, b_sem, f_sem,
+    gs_v, gr_v, gm_v, rs_v, rr_v, k0_v, k1_v, fs_v, fr_v,
+    in_sem, e_sem, s_sem, lz_sem, z_sem, lx_sem, x_sem, b_sem, f_sem,
     wy_sem, wx_sem, wc_sem, g_sem, r_sem, n_sem,
 ):
     mark = Marks()
@@ -100,6 +100,8 @@
                           {X: x_to[d]}) for d in range(1, nx)}
     b_copies = {d: remote(zb_v.at[z_to[d]], inc_v.at[z], b_sem.at[0], b_sem.at[d],
                           {Z: z_to[d]}) for d in range(1, nz)}
+    b_to = [remote(zb_v.at[j], inc_v.at[z], b_sem.at[0], b_sem.at[(j + nz - z) % nz], {Z: j})
+            for j in range(nz)]
     b_all = remote(zb_v.at[most], inc_v.at[most], b_sem.at[0], b_sem.at[1], other)
     f_copies = {d: remote(inc_v.at[z_from[d]], inc_v.at[z_from[d]], f_sem.at[0],
                           f_sem.at[1], other) for d in range(nz)}
@@ -400,8 +402,8 @@
         for j in range(nz):
             zb_v[j] = (pre_v[j] + enter * jnp.exp(log)).astype(BF16)
             log = log + lz_v[j]
-        for d in far_first(nz):
-            b_copies[d].start()
+        for j in range(nz):
+            pl.when(z != j)(b_to[j].start)
         inc_v[z] = zb_v[z]
         f_copies[0].start()
 
@@ -501,22 +503,20 @@
         k0_v[s, j] = pair_sum(s, j, y)
     mark("sum")
 
-    def put(src, row):
-        pltpu.make_async_copy(src, out_hbm.at[pl.ds(row, SPAN), :], out_sem.at[0]).start()
-
     for i, (s, j) in enumerate(order):
         mark(f"w_r{i}")
         r_copies[i].wait_recv()
         mark(f"sum{i}")
         fs_v[s, j] = (k1_v[s, j] + rr_v[s, j, 1].astype(F32)).astype(BF16)
         n_copies[i].start()
-        o_v[s, j] = (k0_v[s, j] + rr_v[s, j, 0].astype(F32)).astype(BF16)
-        put(o_v.at[s, j], start_row(s, True, j))
+        out_ref[pl.ds(start_row(s, True, j), SPAN), :] = (
+            k0_v[s, j] + rr_v[s, j, 0].astype(F32)
+        ).astype(BF16)
     mark("last")
     for i, (s, j) in enumerate(order):
         mark(f"w_n{i}")
         n_copies[i].wait_recv()
-        put(fr_v.at[s, j], start_row(s, False, j))
+        out_ref[pl.ds(start_row(s, False, j), SPAN), :] = fr_v[s, j]
 
     mark("drain")
 
@@ -540,7 +540,6 @@
 
     for buf, sem in ((gs_v, g_sem), (rs_v, r_sem), (fs_v, n_sem)):
         remote(buf, buf, sem.at[chunks * 2], sem.at[0], other).wait_send()
-    pltpu.make_async_copy(v_v, out_hbm, out_sem.at[0]).wait()
     mark(None)
 
 
@@ -570,8 +569,8 @@
         vmem(blocks, BF16), vmem(blocks, BF16), vmem(blocks, BF16),
         vmem((2, chunks, 2, SPAN, width), BF16), vmem((2, chunks, 2, SPAN, width), BF16),
         vmem(blocks, F32), vmem(blocks, F32),
-        vmem(blocks, BF16), vmem(blocks, BF16), vmem(blocks, BF16),
-        dma((7,)), dma((1,)), dma((2,)), dma((2,)), dma((2,)), dma((2,)),
+        vmem(blocks, BF16), vmem(blocks, BF16),
+        dma((7,)), dma((2,)), dma((2,)), dma((2,)), dma((2,)),
         dma((2, nx - 1)), dma((2, nx - 1)), dma((nz,)), dma((2,)),
         dma((5,)), dma((5,)), dma((3,)),
         dma((2 * chunks + 1,)), dma((2 * chunks + 1,)), dma((2 * chunks + 1,)),
@@ -580,12 +579,13 @@
         functools.partial(body, nx, nz, tok, width),
         out_shape=jax.ShapeDtypeStruct((tok, width), BF16),
         in_specs=[any_spec] * 7,
-        out_specs=any_spec,
+        out_specs=pl.BlockSpec(memory_space=pltpu.VMEM),
         scratch_shapes=scratch,
         compiler_params=pltpu.CompilerParams(
-            collective_id=0, has_side_effects=True, vmem_limit_bytes=67043328
+            collective_id=0, has_side_effects=True, vmem_limit_bytes=40 * 2**20
         ),
-    )(queries, key_vectors, values, log_gate, out_gate, norm_gain.reshape(1, DV), out_weight)
+    )(*[pltpu.with_memory_space_constraint(v, pltpu.HBM) for v in (
+        queries, key_vectors, values, log_gate, out_gate, norm_gain.reshape(1, DV), out_weight)])
 
 
 def build(devices, nx, nz):

time: 41.4 us -> 38.9 us (0.940)
  Pallas kernels: 39.4 us -> 37.9 us
  local copies, waits for them, and re-layouts: 1.87 us -> 0.8 us
    pallas_call x1, Pallas kernels: 39.4 us -> 37.9 us  [shards(): pl.pallas_call(functools.partial(body, nx, nz, tok, width), out_shape=jax...]
    unnamed x1, local copies, waits for them, and re-layouts: 1.87 us -> 0.8 us
where the time goes in v4:
time: 38.9 us; the launch traced here: 38.7 us
  Pallas kernels  37.9 us (97%)
  local copies, waits for them, and re-layouts  0.8 us (2%)
    pallas_call x1, Pallas kernels, shards(): pl.pallas_call(functools.partial(body, nx, nz, tok, width), out_shape=jax...  37.9 us
    unnamed x1, local copies, waits for them, and re-layouts  0.8 us

profile of v4, /device:TPU:2, one launch (start us, length us, event | category | flops | bytes accessed | tf_op | source)
XLA Modules:
  0.0 38.7 jit_solution(10409416282020603683)
XLA Ops:
  0.0 37.9 %shard_map.73 = bf16[512,512]{1,0:T(8,128)(2,1)S(1)} custom-call(bf16[512,256]{1,0:T(8,128)(2,1)} %q_hbm.1, bf16[512,256]{1,0:T(8,128)(2,1)} %k_hbm.1, bf16[512,512]{1,0:T(8,128)(2,1)} %v_hbm.1, bf16[512,256]{1,0:T(8,128)(2,1)} %g_hbm.1, bf16[512,512]{1,0:T(8,128)(2,1)} %og_hbm.1, f32[1,512]{1,0:T(1,128)} %bitcast.1, bf16[512,2048]{1,0:T(8,128)(2,1)} %w_hbm.1), custom_call_target="tpu_custom_call" | custom-call | tf_op jit(solution)/shard_map/pallas_call | solution.py:578
  37.9 0.8 %copy.9 = bf16[512,512]{1,0:T(8,128)(2,1)} copy(bf16[512,512]{1,0:T(8,128)(2,1)S(1)} %shard_map.73) | data formatting | bytes 1048576

commit v5 on v4

--- a/solution.py
+++ b/solution.py
@@ -376,8 +376,9 @@
             pre_v[j] = run
             run = run * jnp.exp(lz_v[j]) + zr_v[j].astype(F32)
         xs_v[...] = run.astype(BF16)
+        pl.when(x == 0)(x_copies[1].start)
         for d in far_first(nx):
-            pl.when(x + d < nx)(x_copies[d].start)
+            pl.when((x + d < nx) & ((x > 0) | (d > 1)))(x_copies[d].start)
 
     mark("w_x")
 
@@ -434,7 +435,7 @@
     mark("gated")
     side_tok = tok // 2
     chunks = side_tok // 2 // SPAN
-    order = [(s, j) for j in range(chunks) for s in (0, 1)]
+    order = [(s, j) for j in range(chunks) for s in (1, 0)]
 
     def start_row(s, own, j):
         lead = jnp.where(s == 0, ((y + 1) // 2) % 2, y // 2)
@@ -508,11 +509,17 @@
         r_copies[i].wait_recv()
         mark(f"sum{i}")
         fs_v[s, j] = (k1_v[s, j] + rr_v[s, j, 1].astype(F32)).astype(BF16)
-        n_copies[i].start()
+        pl.when(c == 0)(n_copies[i].start)
         out_ref[pl.ds(start_row(s, True, j), SPAN), :] = (
             k0_v[s, j] + rr_v[s, j, 0].astype(F32)
         ).astype(BF16)
     mark("last")
+
+    @pl.when(c == 1)
+    def _():
+        for copy in n_copies:
+            copy.start()
+
     for i, (s, j) in enumerate(order):
         mark(f"w_n{i}")
         n_copies[i].wait_recv()

time: 38.9 us -> 38.5 us (0.990); the launches traced: 38.7 us -> 37.8 us
  Pallas kernels: 37.9 us -> 37 us
    pallas_call x1, Pallas kernels: 37.9 us -> 37 us  [shards(): pl.pallas_call(functools.partial(body, nx, nz, tok, width), out_shape=jax...]
where the time goes in v5:
time: 38.5 us; the launch traced here: 37.8 us
  Pallas kernels  37 us (96%)
  local copies, waits for them, and re-layouts  0.8 us (2%)
    pallas_call x1, Pallas kernels, shards(): pl.pallas_call(functools.partial(body, nx, nz, tok, width), out_shape=jax...  37 us
    unnamed x1, local copies, waits for them, and re-layouts  0.8 us

profile of v5, /device:TPU:2, one launch (start us, length us, event | category | flops | bytes accessed | tf_op | source)
XLA Modules:
  0.0 37.8 jit_solution(2355000035347901987)
XLA Ops:
  0.0 37.0 %shard_map.73 = bf16[512,512]{1,0:T(8,128)(2,1)S(1)} custom-call(bf16[512,256]{1,0:T(8,128)(2,1)} %q_hbm.1, bf16[512,256]{1,0:T(8,128)(2,1)} %k_hbm.1, bf16[512,512]{1,0:T(8,128)(2,1)} %v_hbm.1, bf16[512,256]{1,0:T(8,128)(2,1)} %g_hbm.1, bf16[512,512]{1,0:T(8,128)(2,1)} %og_hbm.1, f32[1,512]{1,0:T(1,128)} %bitcast.1, bf16[512,2048]{1,0:T(8,128)(2,1)} %w_hbm.1), custom_call_target="tpu_custom_call" | custom-call | tf_op jit(solution)/shard_map/pallas_call | solution.py:585
  37.0 0.8 %copy.9 = bf16[512,512]{1,0:T(8,128)(2,1)} copy(bf16[512,512]{1,0:T(8,128)(2,1)S(1)} %shard_map.73) | data formatting | bytes 1048576

commit v6 on v5

--- a/solution.py
+++ b/solution.py
@@ -361,16 +361,8 @@
         for d in range(1, nx):
             pl.when(x + d < nx)(lx_copies[d].start)
 
-    mark("w_z")
-
-    @pl.when(c == 1)
-    def _():
         z_all.wait_recv()
 
-    mark("zprefix")
-
-    @pl.when(c == 1)
-    def _():
         run = jnp.zeros((piece, DK), F32)
         for j in range(nz):
             pre_v[j] = run
@@ -380,19 +372,11 @@
         for d in far_first(nx):
             pl.when((x + d < nx) & ((x > 0) | (d > 1)))(x_copies[d].start)
 
-    mark("w_x")
-
-    @pl.when(c == 1)
-    def _():
         for d in range(1, nx):
             pl.when(x >= d)(lx_copies[d].wait_recv)
         for d in near_first(nx):
             pl.when(x >= d)(x_copies[d].wait_recv)
 
-    mark("xprefix")
-
-    @pl.when(c == 1)
-    def _():
         ent_v[...] = jnp.zeros_like(ent_v)
         for j in range(nx - 1):
             @pl.when(j < x)
@@ -408,10 +392,6 @@
         inc_v[z] = zb_v[z]
         f_copies[0].start()
 
-    mark("w_b")
-
-    @pl.when(c == 1)
-    def _():
         for d in near_first(nz):
             b_copies[d].wait_recv()
             f_copies[d].start()

time: 38.5 us -> 38.5 us (level)
  no operation moved by 1% of the time
where the time goes in v6:
time: 38.5 us; the launch traced here: 37.8 us
  Pallas kernels  37 us (96%)
  local copies, waits for them, and re-layouts  0.8 us (2%)
    pallas_call x1, Pallas kernels, shards(): pl.pallas_call(functools.partial(body, nx, nz, tok, width), out_shape=jax...  37 us
    unnamed x1, local copies, waits for them, and re-layouts  0.8 us

profile of v6, /device:TPU:2, one launch (start us, length us, event | category | flops | bytes accessed | tf_op | source)
XLA Modules:
  0.0 37.8 jit_solution(2355000035347901987)
XLA Ops:
  0.0 37.0 %shard_map.73 = bf16[512,512]{1,0:T(8,128)(2,1)S(1)} custom-call(bf16[512,256]{1,0:T(8,128)(2,1)} %q_hbm.1, bf16[512,256]{1,0:T(8,128)(2,1)} %k_hbm.1, bf16[512,512]{1,0:T(8,128)(2,1)} %v_hbm.1, bf16[512,256]{1,0:T(8,128)(2,1)} %g_hbm.1, bf16[512,512]{1,0:T(8,128)(2,1)} %og_hbm.1, f32[1,512]{1,0:T(1,128)} %bitcast.1, bf16[512,2048]{1,0:T(8,128)(2,1)} %w_hbm.1), custom_call_target="tpu_custom_call" | custom-call | tf_op jit(solution)/shard_map/pallas_call | solution.py:565
  37.0 0.8 %copy.9 = bf16[512,512]{1,0:T(8,128)(2,1)} copy(bf16[512,512]{1,0:T(8,128)(2,1)S(1)} %shard_map.73) | data formatting | bytes 1048576
